TPU v7x, 512 devices: a 4x2x32 block of a 4x8x32 slice. The times are simulated.
512 devices in a mesh: groups: 2 (over y), ep: 64 (over z, core), tp: 4 (over x).
Axes of the slice: x: 4, y: 2, z: 32, core: 2. Of those that a mesh axis runs over, the one named last changes fastest.
The devices are a block of a 4x8x32 slice.
Arguments:
- hidden: bfloat16 [8192, 2880], P(('groups', 'ep')), parts along dimension 0, may hold values from -6 to 6
- route_experts: int32 [8192, 4], P(('groups', 'ep')), parts along dimension 0, may hold values from 0 to 63, all different within a row; in each aligned block of 64 rows (0 to 63, 64 to 127, ...) at most 8 rows name the same one
- route_weight: float32 [8192, 4], P(('groups', 'ep')), parts along dimension 0, may hold values from 0.1 to 0.6
- norm_gain: bfloat16 [2880], replicated, may hold values from 0.099609375 to 1.8984375
- gate_up_codes: int32 [64, 360, 5120], P('ep', None, 'tp'), may hold values from -2147483648 to 2147483646
- gate_up_scales: bfloat16 [64, 90, 5120], P('ep', None, 'tp'), as said below
- gate_up_bias: bfloat16 [64, 5120], P('ep', 'tp'), may hold values from -3 to 3
- down_codes: int32 [64, 2560, 360], P('ep', 'tp'), may hold values from -2147483648 to 2147483646
- down_scales: bfloat16 [64, 80, 2880], P('ep', 'tp'), as said below
- down_bias: bfloat16 [64, 2880], P('ep', 'tp'), may hold values from -3 to 3
Outputs:
- layer_out: bfloat16 [8192, 2880], P(('groups', 'ep'), 'tp'), parts along dimension 0
There are 2 independent parts, one for each index of `groups`. A program takes and returns all parts, laid end to end along the dimension named above; an argument that names none is the same for every part. Nothing has to cross between parts.
Inputs may be any that keep to these rules, and one draw needn't show every extreme that they name: `route_experts`: each row names 4 different experts. In each aligned block of 64 rows no expert is named by more than 8 rows, and in some blocks one expert is named by exactly 8 rows. `gate_up_scales`: every scale is a power of two. `down_scales`: every scale is a power of two.
All inputs are finite; a program needn't handle non-finite values.
Results may differ from a plain program's by a relative error of at most 0.013.
Values may be sent and summed in bfloat16 or wider, within the bound.
A program may use at most 128 MiB of HBM per device.

v0:
```python
import jax
import jax.numpy as jnp
from jax import lax
from jax.sharding import PartitionSpec as P


def cut_along(shard, dim, count):
    lengths = shard.shape
    pieces = shard.reshape(*lengths[:dim], count, lengths[dim] // count, *lengths[dim + 1 :])
    return jnp.moveaxis(pieces, dim, 0)


def sent_and_summed(shard, axis, dim):
    pieces = cut_along(shard, dim, lax.axis_size(axis))
    arrived = lax.all_to_all(pieces, axis, split_axis=0, concat_axis=0, tiled=True)
    return arrived.astype(jnp.float32).sum(axis=0)


def decode_nibble(nibble):
    magnit = nibble & 7
    exponent = jnp.maximum(jnp.right_shift(magnit, 1) - 1, 0)
    doubled = jnp.where(magnit < 2, magnit, jnp.left_shift(2 + (magnit & 1), exponent))
    signed_val = doubled.astype(jnp.float32) * 0.5
    return jnp.where(nibble >= 8, -signed_val, signed_val)


def unpack_weights(packed, scaling):
    row_count = packed.shape[0]
    shifts = jnp.arange(8, dtype=jnp.int32) * 4
    nibble = jnp.right_shift(packed[:, :, None], shifts[None, None, :]) & 15
    nibble = nibble.reshape(row_count, packed.shape[1] * 8)
    signed_val = decode_nibble(nibble)
    signed_val = (
        signed_val.reshape(row_count // 32, 32, -1) * scaling.astype(jnp.float32)[:, None, :]
    )
    return signed_val.reshape(row_count, -1).astype(jnp.bfloat16)


def unpack_rows(packed, scaling):
    row_count = packed.shape[0] * 8
    shifts = jnp.arange(8, dtype=jnp.int32) * 4
    nibble = jnp.right_shift(packed[:, None, :], shifts[None, :, None]) & 15
    nibble = nibble.reshape(row_count, packed.shape[1])
    signed_val = decode_nibble(nibble)
    signed_val = (
        signed_val.reshape(row_count // 32, 32, -1) * scaling.astype(jnp.float32)[:, None, :]
    )
    return signed_val.reshape(row_count, -1).astype(jnp.bfloat16)


def rms_normed(hidden, norm_gain):
    widened = hidden.astype(jnp.float32)
    mean_square = jnp.mean(widened * widened, axis=-1, keepdims=True)
    scaled = widened * lax.rsqrt(mean_square + 1e-05) * norm_gain.astype(jnp.float32)
    return scaled.astype(jnp.bfloat16)


def shards(
    hidden,
    route_experts,
    route_weight,
    norm_gain,
    gate_up_codes,
    gate_up_scales,
    gate_up_bias,
    down_codes,
    down_scales,
    down_bias,
):
    ep_count = lax.axis_size("ep")
    tp_count = lax.axis_size("tp")
    tp_rank = lax.axis_index("tp")
    tok_count, model_width = hidden.shape
    top_count = route_experts.shape[1]
    capacity = min(tok_count, max(tp_count, 2 * tok_count * top_count // ep_count))
    normed = rms_normed(hidden, norm_gain)
    flat_routes = route_experts.reshape(-1)
    onehot = (flat_routes[:, None] == jnp.arange(ep_count, dtype=jnp.int32)[None, :]).astype(
        jnp.int32
    )
    before = jnp.cumsum(onehot, axis=0) - onehot
    slot_of = jnp.sum(before * onehot, axis=1)
    target = (flat_routes * capacity + slot_of).reshape(tok_count, top_count)
    columns = jnp.arange(ep_count * capacity, dtype=jnp.int32)
    matches = target[:, :, None] == columns[None, None, :]
    placing = jnp.any(matches, axis=1).astype(jnp.bfloat16)
    weighting = jnp.sum(jnp.where(matches, route_weight[:, :, None], 0.0), axis=1)
    outgoing = lax.dot_general(
        placing, normed, (((0,), (0,)), ((), ())), preferred_element_type=jnp.float32
    ).astype(jnp.bfloat16)
    outgoing = outgoing.reshape(ep_count, capacity, model_width)
    gate_up_weight = unpack_rows(gate_up_codes[0], gate_up_scales[0])
    down_weight = unpack_weights(down_codes[0], down_scales[0])
    slot_share = capacity // tp_count
    own_slots = lax.dynamic_slice_in_dim(outgoing, tp_rank * slot_share, slot_share, 1)
    arrived = lax.all_to_all(own_slots, "ep", split_axis=0, concat_axis=0, tiled=True)
    complete = lax.all_gather(arrived, "tp", axis=1, tiled=True)
    source_count, item_count, _ = complete.shape
    flat_rows = complete.reshape(source_count * item_count, model_width)
    projected = jnp.dot(
        flat_rows, gate_up_weight, preferred_element_type=jnp.float32
    ) + gate_up_bias[0].astype(jnp.float32)
    gate_part = jnp.minimum(projected[:, 0::2], 7.0)
    upward = jnp.clip(projected[:, 1::2], -7.0, 7.0)
    activated = (gate_part * jax.nn.sigmoid(1.702 * gate_part) * (upward + 1.0)).astype(
        jnp.bfloat16
    )
    partial_value = jnp.dot(activated, down_weight, preferred_element_type=jnp.float32)
    partial_value = partial_value.astype(jnp.bfloat16).astype(jnp.float32)
    partial_value = partial_value.reshape(source_count, item_count, model_width)
    summed = sent_and_summed(partial_value.astype(jnp.bfloat16), "tp", 2)
    answered = (summed + down_bias[0].astype(jnp.float32)).astype(jnp.bfloat16)
    came_back = lax.all_to_all(answered, "ep", split_axis=0, concat_axis=0, tiled=True)
    quarter = model_width // tp_count
    own_cols = lax.dynamic_slice_in_dim(hidden, tp_rank * quarter, quarter, 1).astype(jnp.float32)
    gathered = came_back.reshape(ep_count * capacity, quarter).astype(jnp.float32)
    layer_out = own_cols + jnp.dot(weighting, gathered, precision=lax.Precision.HIGHEST)
    return layer_out.astype(jnp.bfloat16)


def solution(mesh):
    placed = (
        P(("groups", "ep"), None),
        P(("groups", "ep"), None),
        P(("groups", "ep"), None),
        P(),
        P("ep", None, "tp"),
        P("ep", None, "tp"),
        P("ep", "tp"),
        P("ep", "tp", None),
        P("ep", "tp", None),
        P("ep", "tp"),
    )
    return jax.shard_map(
        shards, mesh=mesh, in_specs=placed, out_specs=P(("groups", "ep"), "tp"), check_vma=False
    )
```

profile of v0, /device:TPU:33, one launch (start us, length us, event | category | flops | bytes accessed | tf_op | source)
XLA Modules:
  0.0 473.0 jit_solution(10467680712080195271)
XLA Ops:
  6.6 0.8 copy.56
  7.6 0.6 reduce-window.6
  8.2 0.2 slice_reduce_fusion
  8.7 0.7 multiply_add_fusion
  9.4 0.1 fusion.38
  9.5 0.7 convert_element_type.113
  10.2 1.2 fusion.31
  11.4 2.1 convolution_convert_fusion.1
  13.5 3.0 copy.60
  16.5 2.6 constant_dynamic-slice_fusion
  19.1 130.1 %all_to_all.15 = bf16[64,2,2880]{2,1,0:T(2,128)(2,1)S(1)} all-to-all(bf16[64,2,2880]{2,1,0:T(2,128)(2,1)S(1)} %constant_dynamic-slice_fusion), channel_id=1, replica_groups=mesh['groups'=2,'ep'=64,'tp'=4] {'ep'}, dimensions={0} | all-to-all | bytes 1474560 | tf_op jit(solution)/shard_map/all_to_all | solution.py:96
  149.2 1.0 copy.61
  150.5 3.5 mul.133
  154.0 9.1 %copy.63 = f32[640,2880]{0,1:T(8,128)} copy(f32[640,2880]{1,0:T(8,128)} %bitcast.99) | data formatting | bytes 14745600 | tf_op jit(solution)/shard_map/mul | solution.py:34
  163.2 6.2 %shift_right_arithmetic.73 = s32[360,8,1280]{2,1,0:T(8,128)} broadcast(s32[360,1280]{1,0:T(8,128)S(1)} %bitcast.103), dimensions={0,2} | broadcast | bytes 16588800 | tf_op jit(solution)/shard_map/shift_right_arithmetic | solution.py:42
  169.4 13.2 %fusion.1 = bf16[90,32,1280]{2,1,0:T(8,128)(2,1)} fusion(f32[90,1280]{1,0:T(8,128)S(1)} %bitcast_convert_fusion, s32[32]{0:T(128)S(1)} %shift_right_arithmetic.76, s32[90,32,1280]{2,1,0:T(8,128)} %bitcast.98), kind=kLoop, calls=%fused_computation.4 | loop fusion | flops 66355200 | bytes 22579328 | tf_op jit(solution)/shard_map/convert_element_type | solution.py:48
  182.6 5.9 %all-gather.2.cloned.1.call-done = bf16[64,8,2880]{2,0,1:T(8,128)(2,1)} async-done(((bf16[64,2,2880]{2,0,1:T(8,128)(2,1)}), bf16[64,8,2880]{2,0,1:T(8,128)(2,1)}) %all-gather.2.cloned.1.call-update) | async-done | bytes 2949136 | tf_op jit(solution)/shard_map/all_gather | solution.py:97
  188.5 9.2 %convolution_add_fusion = f32[512,1280]{1,0:T(8,128)S(1)} fusion(bf16[2880,1280]{1,0:T(8,128)(2,1)} %bitcast.101, bf16[64,8,2880]{2,0,1:T(8,128)(2,1)} %all-gather.2.cloned.1.call-done, f32[1280]{0:T(1024)S(1)} %convert_reduce_fusion.1), kind=kOutput, calls=%fused_computation.35 | convolution fusion | flops 3775528960 | bytes 12948480 | tf_op jit(solution)/shard_map/dot_general | solution.py:100
  197.7 46.3 %slice.14 = f32[512,640]{1,0:T(8,128)} slice(f32[512,1280]{1,0:T(8,128)S(1)} %convolution_add_fusion), slice={[0:512:1], [0:1280:2]} | slice | bytes 2621440 | tf_op jit(solution)/shard_map/slice | solution.py:103
  244.0 46.0 %slice.15 = f32[512,640]{1,0:T(8,128)} slice(f32[512,1280]{1,0:T(8,128)S(1)} %convolution_add_fusion), slice={[0:512:1], [1:1280:2]} | slice | bytes 2621440 | tf_op jit(solution)/shard_map/slice | solution.py:104
  290.0 9.1 %convolution_convert_fusion = bf16[512,2880]{0,1:T(8,128)(2,1)S(1)} fusion(f32[640,2880]{0,1:T(8,128)} %copy.63, s32[2880]{0:T(1024)S(1)} %shift_right_arithmetic.84, s32[640,360]{0,1:T(8,128)} %bitcast.104, f32[512,640]{1,0:T(8,128)} %slice.15, f32[512,640]{1,0:T(8,128)} %slice.14), kind=kOutput, calls=%fused_computation.33 | convolution fusion | flops 1925365760 | bytes 13876480 | tf_op jit(solution)/shard_map/dot_general | solution.py:108
  299.1 3.0 copy.64
  302.1 7.6 %convert_element_type.127 = bf16[64,8,4,720]{3,2,1,0:T(4,128)(2,1)S(1)} reshape(bf16[512,2880]{1,0:T(8,128)(2,1)} %copy.64) | data formatting | bytes 5898240 | tf_op jit(solution)/shard_map/convert_element_type | solution.py:111
  309.7 2.1 copy.65
  311.7 3.9 all-to-all-start.1
  315.7 36.7 %all-to-all-done.1 = bf16[4,64,8,720]{3,2,1,0:T(8,128)(2,1)S(1)} async-done(((bf16[4,64,8,720]{3,2,1,0:T(8,128)(2,1)}), bf16[4,64,8,720]{3,2,1,0:T(8,128)(2,1)S(1)}, u32[]{:S(2)}, u32[]{:S(2)}) %all-to-all-start.1) | async-done | bytes 2949152 | tf_op jit(solution)/shard_map/all_to_all | solution.py:15
  352.4 0.4 convert_reduce_fusion
  352.8 1.0 add_convert_fusion
  353.8 25.4 %all-to-all-start.2 = ((bf16[64,8,720]{2,1,0:T(8,128)(2,1)}), bf16[64,8,720]{2,1,0:T(8,128)(2,1)S(1)}, u32[]{:S(2)}, u32[]{:S(2)}) async-start(bf16[64,8,720]{2,1,0:T(8,128)(2,1)} %add_convert_fusion), calls=%async_computation.2 | async-start | bytes 1572864 | tf_op jit(solution)/shard_map/all_to_all | solution.py:113
  379.3 0.1 select_reduce_fusion
  379.4 84.7 %all-to-all-done.2 = bf16[64,8,720]{2,1,0:T(8,128)(2,1)S(1)} async-done(((bf16[64,8,720]{2,1,0:T(8,128)(2,1)}), bf16[64,8,720]{2,1,0:T(8,128)(2,1)S(1)}, u32[]{:S(2)}, u32[]{:S(2)}) %all-to-all-start.2) | async-done | bytes 737312 | tf_op jit(solution)/shard_map/all_to_all | solution.py:113
  464.1 2.1 fusion.29
  (32 shorter events, 1.0 us)
Async XLA Ops:
  6.5 182.0 %all-gather.2.cloned.1.call-start = ((), (), s32[]{:S(2)}) async-start(), calls=%async_computation.3 | async-start | bytes 3768320 | tf_op jit(solution)/shard_map/all_gather | solution.py:97
  11.4 139.1 %copy-start.2 = (bf16[1,20,2880]{2,1,0:T(8,128)(2,1)S(1)}, bf16[1,20,2880]{2,1,0:T(8,128)(2,1)}, u32[]{:S(2)}) copy-start(bf16[1,20,2880]{2,1,0:T(8,128)(2,1)} %param.18) | copy-start | bytes 345604
  154.0 9.1 %copy-start.3 = (bf16[1,1280]{1,0:T(2,128)(2,1)S(1)}, bf16[1,1280]{1,0:T(2,128)(2,1)}, u32[]{:S(2)}) copy-start(bf16[1,1280]{1,0:T(2,128)(2,1)} %param.16) | copy-start | bytes 7684
  154.0 9.1 %copy-start.1 = (bf16[1,90,1280]{2,1,0:T(8,128)(2,1)S(1)}, bf16[1,90,1280]{2,1,0:T(8,128)(2,1)}, u32[]{:S(2)}) copy-start(bf16[1,90,1280]{2,1,0:T(8,128)(2,1)} %param.15) | copy-start | bytes 691204
  154.0 9.2 %copy-start = (s32[1,360,1280]{2,1,0:T(8,128)S(1)}, s32[1,360,1280]{2,1,0:T(8,128)}, u32[]{:S(2)}) copy-start(s32[1,360,1280]{2,1,0:T(8,128)} %param.14) | copy-start | bytes 5529604
  309.6 6.0 %copy-start.4 = (bf16[1,720]{1,0:T(2,128)(2,1)S(1)}, bf16[1,720]{1,0:T(2,128)(2,1)}, u32[]{:S(2)}) copy-start(bf16[1,720]{1,0:T(2,128)(2,1)} %param.19) | copy-start | bytes 4324
  311.7 67.5 %copy-start.5 = (f32[64,4]{0,1:T(4,128)S(1)}, f32[64,4]{0,1:T(4,128)}, u32[]{:S(2)}) copy-start(f32[64,4]{0,1:T(4,128)} %param.12) | copy-start | bytes 3076
  311.7 40.7 %all-to-all-start.1 = ((bf16[4,64,8,720]{3,2,1,0:T(8,128)(2,1)}), bf16[4,64,8,720]{3,2,1,0:T(8,128)(2,1)S(1)}, u32[]{:S(2)}, u32[]{:S(2)}) async-start(bf16[4,64,8,720]{3,2,1,0:T(8,128)(2,1)} %copy.65), calls=%async_computation.1 | async-start | bytes 6291456 | tf_op jit(solution)/shard_map/all_to_all | solution.py:15
  353.8 110.2 %all-to-all-start.2 = ((bf16[64,8,720]{2,1,0:T(8,128)(2,1)}), bf16[64,8,720]{2,1,0:T(8,128)(2,1)S(1)}, u32[]{:S(2)}, u32[]{:S(2)}) async-start(bf16[64,8,720]{2,1,0:T(8,128)(2,1)} %add_convert_fusion), calls=%async_computation.2 | async-start | bytes 1572864 | tf_op jit(solution)/shard_map/all_to_all | solution.py:113
Sparse Core Ops, SparseCore 0:
  150.4 38.1 all-gather.1
where the time goes:
time: 475 us; the launch traced here: 473 us
  local copies, waits for them, and re-layouts  132 us (28%)
  blocking collectives  130 us (27%)
  waiting for transfers between devices  127 us (27%)
  starting transfers between devices  29.3 us (6%)
  matrix products  22.4 us (5%)
  other arithmetic  18.3 us (4%)
  between operations  13.6 us (3%)
    all_to_all x1, blocking collectives, shards(): lax.all_to_all(own_slots, 'ep', split_axis=0, concat_axis=0, tiled=True)  130 us
    all_to_all x1, waiting for transfers between devices, shards(): lax.all_to_all(answered, 'ep', split_axis=0, concat_axis=0, tiled=True)  84.7 us
    slice x1, local copies, waits for them, and re-layouts, shards(): gate_part = jnp.minimum(projected[:, 0::2], 7.0)  46.3 us
    slice x1, local copies, waits for them, and re-layouts, shards(): upward = jnp.clip(projected[:, 1::2], -7.0, 7.0)  46 us
    all_to_all x1, waiting for transfers between devices, sent_and_summed(): lax.all_to_all(pieces, axis, split_axis=0, concat_axis=0, tiled=True)  36.7 us
    all_to_all x1, starting transfers between devices, shards(): lax.all_to_all(answered, 'ep', split_axis=0, concat_axis=0, tiled=True)  25.4 us
    convert_element_type x1, other arithmetic, unpack_rows(): return signed_val.reshape(row_count, -1).astype(jnp.bfloat16)  13.2 us
    mul x2, local copies, waits for them, and re-layouts, unpack_weights(): signed_val.reshape(row_count // 32, 32, -1)  12.6 us
  transfers between devices with their start and end apart: 3, of which 3 were waited for; matrix products, arithmetic and copies ran while one was open for 7% of the time, Pallas kernels for 0%

commit v1 on v0

v1 whole, which is shorter than its diff:
```python
import functools

import jax
import jax.numpy as jnp
from jax import lax
from jax.experimental import pallas as pl
from jax.experimental.pallas import tpu as pltpu
from jax.sharding import PartitionSpec as P

CAP = 8
CHUNKS = 2
F32 = jnp.float32
BF16 = jnp.bfloat16


def dot(a, b):
    return jnp.dot(a, b, preferred_element_type=F32)


def iota(shape, dim):
    return lax.broadcasted_iota(jnp.int32, shape, dim)


def neighbours(ep, tp):
    me = lax.axis_index("ep")
    core = lax.rem(me, 2)
    col = lax.axis_index("tp")
    return dict(
        me=me,
        up=lax.rem(me + 2, ep),
        down=lax.rem(me + ep - 2, ep),
        pal=me + 1 - 2 * core,
        col=col,
        right=lax.rem(col + 1, tp),
        left=lax.rem(col + tp - 1, tp),
        across=lax.rem(col + 2, tp),
    )


def greet(at):
    barrier = pltpu.get_barrier_semaphore()
    for place in ({"ep": at["up"]}, {"ep": at["down"]}, {"ep": at["pal"]}, {"tp": at["right"]}, {"tp": at["left"]}):
        pl.semaphore_signal(barrier, inc=1, device_id=place, device_id_type=pl.DeviceIdType.MESH)
    pl.semaphore_wait(barrier, 5)


def remote(src, dst, send, recv, place):
    return pltpu.make_async_remote_copy(
        src_ref=src, dst_ref=dst, send_sem=send, recv_sem=recv, device_id=place, device_id_type=pl.DeviceIdType.MESH
    )


def dispatch_kernel(
    ep, tp, top, meta_at, block_ref, rows_ref, mix_ref, held, handed, own_sem, zs, zr, ds, dr, xs, xr
):
    pairs = held.shape[0]
    tokens = held.shape[2]
    part = tokens // CHUNKS
    at = neighbours(ep, tp)
    greet(at)
    first = pltpu.make_async_copy(block_ref, held.at[0, 0], own_sem)
    first.start()
    first.wait()

    def piece(pair, side, h):
        return held.at[pair, side, pl.ds(h * part, part)]

    def hop(s, side, h):
        src = piece(0, 0, h) if isinstance(s, int) and s == 1 else piece(s - 1, side, h)
        place = {"ep": at["up"] if side == 0 else at["down"]}
        return remote(src, piece(s, side, h), zs.at[s, side, h], zr.at[s, side, h], place)

    def last_hop(side, h):
        place = {"ep": at["up"] if side == 0 else at["down"]}
        return remote(
            piece(pairs - 1, side, h), piece(0, 1, h), zs.at[0, side, h], zr.at[0, side, h], place
        )

    def last_side(h):
        return 0 if h < CHUNKS // 2 else 1

    def tile(col, pair, p):
        return rows_ref.at[col, pair * 2 + p]

    def to_pal(pair):
        return remote(
            handed.at[pair], tile(at["col"], pair, 1), ds.at[pair], dr.at[pair], {"ep": at["pal"]}
        )

    def across_right(pair, p):
        return remote(
            tile(at["col"], pair, p), tile(at["col"], pair, p), xs.at[pair * 2 + p, 0],
            xr.at[pair * 2 + p, 0], {"tp": at["right"]},
        )

    def across_left(pair, p):
        return remote(
            tile(at["col"], pair, p), tile(at["col"], pair, p), xs.at[pair * 2 + p, 1],
            xr.at[pair * 2 + p, 1], {"tp": at["left"]},
        )

    def from_left(pair, p):
        return remote(
            tile(at["left"], pair, p), tile(at["left"], pair, p), xs.at[pair * 2 + p, 0],
            xr.at[pair * 2 + p, 0], {"tp": at["right"]},
        )

    def from_right(pair, p):
        return remote(
            tile(at["right"], pair, p), tile(at["right"], pair, p), xs.at[pair * 2 + p, 1],
            xr.at[pair * 2 + p, 1], {"tp": at["left"]},
        )

    def relay(pair, p):
        col, place = (at["left"], at["right"]) if p == 0 else (at["right"], at["left"])
        return remote(
            tile(col, pair, p), tile(col, pair, p), xs.at[pair * 2 + p, 2], xr.at[pair * 2 + p, 2],
            {"tp": place},
        )

    def relayed(pair, p):
        return remote(
            tile(at["across"], pair, p), tile(at["across"], pair, p), xs.at[pair * 2 + p, 2],
            xr.at[pair * 2 + p, 2], {"tp": at["right"]},
        )

    for h in range(CHUNKS):
        for side in range(2):
            hop(1, side, h).start()

    both = 2 * tokens
    lane = iota((both, 128), 1)
    ks, ls = iota((128, 128), 0), iota((128, 128), 1)
    own_cols = (ls < 16).astype(BF16)
    pal_cols = ((ls >= 16) & (ls < 32)).astype(BF16)
    ti, tj = iota((both, both), 0), iota((both, both), 1)
    earlier = ((tj < ti) & ((ti < tokens) == (tj < tokens))).astype(BF16)
    wanted = lax.rem(lane, 16) - jnp.where(iota((both, 128), 0) >= tokens, 8, 0)
    wanted = wanted.astype(F32)
    id_lanes = (lane >= meta_at) & (lane < meta_at + top)
    own_id = at["me"].astype(F32)
    pal_id = at["pal"].astype(F32)

    def select(pair):
        width = held.shape[3]
        block = held[pair].reshape(both, width)
        meta = block[:, width - 128 :].astype(F32)
        weights = pltpu.roll(meta, 128 - top, axis=1)
        is_own = id_lanes & (meta == own_id)
        is_pal = id_lanes & (meta == pal_id)
        match = dot(jnp.where(is_own, 1.0, 0.0).astype(BF16), own_cols) + dot(
            jnp.where(is_pal, 1.0, 0.0).astype(BF16), pal_cols
        )
        weight = dot(jnp.where(is_own, weights, 0.0).astype(BF16), own_cols) + dot(
            jnp.where(is_pal, weights, 0.0).astype(BF16), pal_cols
        )
        slot = dot(earlier, match.astype(BF16))
        placed = (match > 0.5) & (slot == wanted)
        mix_ref[pair] = jnp.where(placed, weight, 0.0).astype(BF16)
        pick = jnp.transpose(jnp.where(placed, 1.0, 0.0))[:32].astype(BF16)
        picked = dot(pick, block).astype(BF16)
        rows_ref[at["col"], pair * 2] = picked[:16]
        handed[pair] = picked[16:]

    def body(u, carry):
        @pl.when(u < pairs - 1)
        def _():
            s = u + 1
            for h in range(CHUNKS):
                for side in range(2):
                    hop(s, side, h).wait_recv()

                    @pl.when(s < pairs - 1)
                    def _():
                        hop(s + 1, side, h).start()

                    if side == last_side(h):

                        @pl.when(s == pairs - 1)
                        def _():
                            last_hop(side, h).start()

        @pl.when(u == pairs - 1)
        def _():
            for h in range(CHUNKS):
                last_hop(last_side(h), h).wait_recv()

        @pl.when(u < pairs)
        def _():
            pair = lax.rem(u + 1, pairs)
            select(pair)
            to_pal(pair).start()
            across_right(pair, 0).start()
            across_left(pair, 0).start()

        @pl.when((u >= 1) & (u < pairs + 1))
        def _():
            pair = lax.rem(u, pairs)
            to_pal(pair).wait_recv()
            across_right(pair, 1).start()
            across_left(pair, 1).start()
            from_left(pair, 0).wait_recv()
            relay(pair, 0).start()

        @pl.when(u >= 2)
        def _():
            pair = lax.rem(u - 1, pairs)
            from_right(pair, 1).wait_recv()
            relay(pair, 1).start()

        return carry

    lax.fori_loop(0, pairs + 2, body, 0)

    def finish(pair, carry):
        from_right(pair, 0).wait_recv()
        from_left(pair, 1).wait_recv()
        to_pal(pair).wait_send()
        for p in range(2):
            relayed(pair, p).wait_recv()
            across_right(pair, p).wait_send()
            across_left(pair, p).wait_send()
            relay(pair, p).wait_send()
        return carry

    lax.fori_loop(0, pairs, finish, 0)

    def sent(s, carry):
        for h in range(CHUNKS):
            for side in range(2):
                hop(s, side, h).wait_send()
        return carry

    lax.fori_loop(1, pairs, sent, 0)
    for h in range(CHUNKS):
        last_hop(last_side(h), h).wait_send()


def dispatch(block, ep, tp, top, meta_at):
    tokens, width = block.shape
    pairs = ep // 4
    dma = pltpu.SemaphoreType.DMA
    vmem = pl.BlockSpec(memory_space=pltpu.VMEM)
    return pl.pallas_call(
        functools.partial(dispatch_kernel, ep, tp, top, meta_at),
        out_shape=(
            jax.ShapeDtypeStruct((tp, 2 * pairs, 16, width), BF16),
            jax.ShapeDtypeStruct((pairs, 2 * tokens, 128), BF16),
        ),
        in_specs=[pl.BlockSpec(memory_space=pl.ANY)],
        out_specs=(vmem, vmem),
        scratch_shapes=[
            pltpu.VMEM((pairs, 2, tokens, width), BF16),
            pltpu.VMEM((pairs, 16, width), BF16),
            dma(()),
            dma((pairs, 2, CHUNKS)),
            dma((pairs, 2, CHUNKS)),
            dma((pairs,)),
            dma((pairs,)),
            dma((2 * pairs, 3)),
            dma((2 * pairs, 3)),
        ],
        compiler_params=pltpu.CompilerParams(
            collective_id=0, has_side_effects=True, vmem_limit_bytes=40 << 20
        ),
        name="dispatch",
    )(block)


def nibble_value(word, shift):
    top_bits = lax.shift_left(word, 28 - shift)
    magnit = lax.shift_right_logical(top_bits, 28) & 7
    doubled = magnit + jnp.maximum(magnit - 4, 0) + 2 * jnp.maximum(magnit - 6, 0)
    value = doubled.astype(F32)
    return jnp.where(top_bits < 0, -value, value)


def experts_kernel(
    rows_ref, codes_ref, scales_ref, bias_ref, low_codes_ref, low_scales_ref, out_ref, upper, lower, act, spread
):
    tp = rows_ref.shape[0]
    width = rows_ref.shape[2]
    columns = codes_ref.shape[1]
    units = upper.shape[0] // tp
    real_units = codes_ref.shape[0] // 2 // tp
    hidden_units = lower.shape[1]
    for q in range(tp):
        upper[q * units + real_units : (q + 1) * units] = jnp.zeros(
            (units - real_units, 16, columns), BF16
        )

    shift = 4 * iota((8, 8, columns), 1)

    def decode(u, carry):
        words = codes_ref[pl.ds(pl.multiple_of(u * 8, 8), 8), :]
        value = nibble_value(jnp.broadcast_to(words[:, None, :], (8, 8, columns)), shift)
        value = value.reshape(2, 32, columns) * (0.5 * scales_ref[u])[:, None, :]
        value = value.reshape(4, 16, columns).astype(BF16)
        for k in range(4):
            unit = 4 * u + k
            upper[unit + (units - real_units) * (unit // real_units)] = value[k]
        return carry

    lax.fori_loop(0, codes_ref.shape[0] // 8, decode, 0)

    word, lanes = iota((128, width), 0), iota((128, width), 1)
    for j in range(8):
        spread[j * 128 : (j + 1) * 128] = (lanes == 8 * word + j).astype(BF16)

    def decode_low(q, carry):
        words = low_codes_ref[:, pl.ds(pl.multiple_of(q * 128, 128), 128)]
        whole = jnp.concatenate([nibble_value(words, 4 * j).astype(BF16) for j in range(8)], axis=1)
        value = dot(whole, spread[...])
        value = value.reshape(hidden_units // 32, 32, width) * (0.5 * low_scales_ref[q])[:, None, :]
        lower[q] = value.reshape(hidden_units, width).astype(BF16)
        return carry

    lax.fori_loop(0, tp, decode_low, 0)

    si, sj = iota((256, 128), 0), iota((256, 128), 1)
    evens = (si == 2 * sj).astype(BF16)

    def project(n, carry):
        at = pl.ds(pl.multiple_of(n * 256, 256), 256)
        total = bias_ref[:, at]
        for q in range(tp):
            weight = upper[q * units : (q + 1) * units, :, at].reshape(units * 16, 256)
            total = total + dot(rows_ref[q], weight)
        gate = jnp.minimum(total, 7.0)
        upward = jnp.clip(pltpu.roll(total, 255, axis=1), -7.0, 7.0)
        value = (gate * jax.nn.sigmoid(1.702 * gate) * (upward + 1.0)).astype(BF16)
        act[:, pl.ds(pl.multiple_of(n * 128, 128), 128)] = dot(value, evens).astype(BF16)
        return carry

    lax.fori_loop(0, columns // 256, project, 0)

    def lower_dot(q, carry):
        out_ref[q] = dot(act[...], lower[q]).astype(BF16)
        return carry

    lax.fori_loop(0, tp, lower_dot, 0)


def experts(rows, codes, scales, bias, low_codes, low_scales):
    tp, row_count, width = rows.shape
    columns = codes.shape[1]
    hidden_units = low_codes.shape[0]
    vmem = pl.BlockSpec(memory_space=pltpu.VMEM)
    return pl.pallas_call(
        experts_kernel,
        out_shape=jax.ShapeDtypeStruct((tp, row_count, width), BF16),
        in_specs=[vmem] * 6,
        out_specs=vmem,
        scratch_shapes=[
            pltpu.VMEM((tp * width // 16, 16, columns), BF16),
            pltpu.VMEM((tp, hidden_units, width), BF16),
            pltpu.VMEM((row_count, hidden_units), BF16),
            pltpu.VMEM((1024, width), BF16),
        ],
        compiler_params=pltpu.CompilerParams(vmem_limit_bytes=56 << 20),
        name="experts",
    )(rows, codes, scales, bias, low_codes, low_scales)


def combine_kernel(
    ep, tp, part_ref, mix_ref, bias_ref, own_ref, out_ref,
    across, summed, staged, direct, outs, handed, moving, leaving, own_sum,
    zs, zr, ds, dr, xs, xr,
):
    pairs = mix_ref.shape[0]
    tokens = moving.shape[2]
    part = tokens // CHUNKS
    at = neighbours(ep, tp)
    greet(at)

    def last_side(h):
        return 1 if h < CHUNKS // 2 else 0

    def up_or_down(side):
        return {"ep": at["up"] if side == 1 else at["down"]}

    def hop(s, side, h):
        src = leaving.at[s, side, pl.ds(h * part, part)]
        dst = moving.at[s - 1, side, pl.ds(h * part, part)]
        return remote(src, dst, zs.at[s - 1, side, h], zr.at[s - 1, side, h], up_or_down(side))

    def first_hop(side, h):
        src = leaving.at[0, 1, pl.ds(h * part, part)]
        dst = moving.at[pairs - 1, side, pl.ds(h * part, part)]
        return remote(src, dst, zs.at[pairs - 1, side, h], zr.at[pairs - 1, side, h], up_or_down(side))

    def far(p):
        return {"tp": at["right"] if p == 0 else at["left"]}

    def near(p):
        return {"tp": at["left"] if p == 0 else at["right"]}

    def two_away(t, p):
        return remote(part_ref.at[at["across"], t], across.at[t], xs.at[t, 0], xr.at[t, 0], far(p))

    def one_away(t, p):
        col = at["left"] if p == 0 else at["right"]
        return remote(part_ref.at[col, t], direct.at[t], xs.at[t, 1], xr.at[t, 1], near(p))

    def onward(t, p):
        return remote(staged.at[t], summed.at[t], xs.at[t, 2], xr.at[t, 2], far(p))

    def to_pal(pair):
        return remote(
            handed.at[pair], outs.at[pair, pl.ds(16, 16)], ds.at[pair], dr.at[pair], {"ep": at["pal"]}
        )

    for h in range(CHUNKS):
        side = 1 - last_side(h)
        moving[pairs - 1, side, h * part : (h + 1) * part] = jnp.zeros((part, moving.shape[3]), BF16)

    def pair_of(u):
        return lax.rem(pairs - u, pairs)

    def body(t, carry):
        @pl.when(t < pairs)
        def _():
            pair = pair_of(t)
            for p in range(2):
                two_away(pair * 2 + p, p).start()
            for p in range(2):
                one_away(pair * 2 + p, p).start()

        @pl.when(t >= 3)
        def _():
            u = t - 3
            pair = pair_of(u)
            to_pal(pair).wait_recv()
            mixed = dot(mix_ref[pair][:, :32], outs[pair])

            @pl.when(u == 0)
            def _():
                own_sum[...] = mixed[:tokens]
                leaving[0, 1] = mixed[tokens:].astype(BF16)
                for h in range(CHUNKS):
                    first_hop(last_side(h), h).start()

            @pl.when(u > 0)
            def _():
                for h in range(CHUNKS):
                    for side in (last_side(h), 1 - last_side(h)):
                        arrival = remote(
                            leaving.at[pair, side, pl.ds(h * part, part)],
                            moving.at[pair, side, pl.ds(h * part, part)],
                            zs.at[pair, side, h],
                            zr.at[pair, side, h],
                            up_or_down(side),
                        )
                        if side == last_side(h):
                            arrival.wait_recv()
                        else:

                            @pl.when(u > 1)
                            def _():
                                arrival.wait_recv()

                        begin = side * tokens + h * part
                        value = mixed[begin : begin + part] + moving[
                            pair, side, h * part : (h + 1) * part
                        ].astype(F32)
                        leaving[pair, side, h * part : (h + 1) * part] = value.astype(BF16)
                        hop(pair, side, h).start()

        @pl.when((t >= 1) & (t < pairs + 1))
        def _():
            pair = pair_of(t - 1)
            for p in range(2):
                tile = pair * 2 + p
                two_away(tile, p).wait_recv()
                col = at["right"] if p == 0 else at["left"]
                staged[tile] = (across[tile].astype(F32) + part_ref[col, tile].astype(F32)).astype(BF16)
                onward(tile, p).start()

        @pl.when((t >= 2) & (t < pairs + 2))
        def _():
            pair = pair_of(t - 2)
            for p in (1, 0):
                tile = pair * 2 + p
                one_away(tile, p).wait_recv()
                onward(tile, p).wait_recv()
                total = (
                    summed[tile].astype(F32)
                    + direct[tile].astype(F32)
                    + part_ref[at["col"], tile].astype(F32)
                    + bias_ref[...]
                ).astype(BF16)
                if p == 1:
                    handed[pair] = total
                    to_pal(pair).start()
                else:
                    outs[pair, :16] = total

        return carry

    lax.fori_loop(0, pairs + 3, body, 0)

    for side in range(2):
        for h in range(CHUNKS):
            hop(1, side, h).wait_recv()
    total = own_ref[...].astype(F32) + own_sum[...] + moving[0, 0].astype(F32) + moving[0, 1].astype(F32)
    out_ref[...] = total[:, : out_ref.shape[1]].astype(BF16)

    def finish(pair, carry):
        to_pal(pair).wait_send()
        for p in range(2):
            two_away(pair * 2 + p, p).wait_send()
            one_away(pair * 2 + p, p).wait_send()
            onward(pair * 2 + p, p).wait_send()
        return carry

    lax.fori_loop(0, pairs, finish, 0)

    def sent(s, carry):
        for h in range(CHUNKS):
            for side in range(2):
                hop(s, side, h).wait_send()
        return carry

    lax.fori_loop(1, pairs, sent, 0)
    for h in range(CHUNKS):
        first_hop(last_side(h), h).wait_send()


def combine(parts, mix, bias, own, quarter, ep):
    tp, tiles, _, width = parts.shape
    pairs = mix.shape[0]
    tokens = own.shape[0]
    dma = pltpu.SemaphoreType.DMA
    vmem = pl.BlockSpec(memory_space=pltpu.VMEM)
    return pl.pallas_call(
        functools.partial(combine_kernel, ep, tp),
        out_shape=jax.ShapeDtypeStruct((tokens, quarter), BF16),
        in_specs=[vmem] * 4,
        out_specs=vmem,
        scratch_shapes=[
            pltpu.VMEM((tiles, 16, width), BF16),
            pltpu.VMEM((tiles, 16, width), BF16),
            pltpu.VMEM((tiles, 16, width), BF16),
            pltpu.VMEM((tiles, 16, width), BF16),
            pltpu.VMEM((pairs, 32, width), BF16),
            pltpu.VMEM((pairs, 16, width), BF16),
            pltpu.VMEM((pairs, 2, tokens, width), BF16),
            pltpu.VMEM((pairs, 2, tokens, width), BF16),
            pltpu.VMEM((tokens, width), F32),
            dma((pairs, 2, CHUNKS)),
            dma((pairs, 2, CHUNKS)),
            dma((pairs,)),
            dma((pairs,)),
            dma((tiles, 3)),
            dma((tiles, 3)),
        ],
        compiler_params=pltpu.CompilerParams(
            collective_id=1, has_side_effects=True, vmem_limit_bytes=40 << 20
        ),
        name="combine",
    )(parts, mix, bias, own)


def rms_normed(hidden, norm_gain):
    widened = hidden.astype(F32)
    mean_square = jnp.mean(widened * widened, axis=-1, keepdims=True)
    scaled = widened * lax.rsqrt(mean_square + 1e-05) * norm_gain.astype(F32)
    return scaled.astype(BF16)


def shards(
    hidden,
    route_experts,
    route_weight,
    norm_gain,
    gate_up_codes,
    gate_up_scales,
    gate_up_bias,
    down_codes,
    down_scales,
    down_bias,
):
    ep = lax.axis_size("ep")
    tp = lax.axis_size("tp")
    col = lax.axis_index("tp")
    tokens, model_width = hidden.shape
    top = route_experts.shape[1]
    quarter = model_width // tp
    width = -(-(quarter + 2 * top) // 128) * 128
    spare = width - quarter
    normed = rms_normed(hidden, norm_gain)
    own_normed = lax.dynamic_slice_in_dim(normed, col * quarter, quarter, 1)
    block = jnp.concatenate(
        [
            own_normed,
            route_experts.astype(BF16),
            route_weight.astype(BF16),
            jnp.zeros((tokens, spare - 2 * top), BF16),
        ],
        axis=1,
    )
    rows, mix = dispatch(block, ep, tp, top, quarter - (width - 128))
    tiles = rows.shape[1]

    codes = gate_up_codes[0]
    columns = codes.shape[1]
    scales = gate_up_scales[0].astype(F32).reshape(-1, 2, columns)
    hidden_units = down_codes.shape[1]
    words = quarter // 8
    low_codes = jnp.pad(down_codes[0].reshape(hidden_units, tp, words), ((0, 0), (0, 0), (0, 128 - words)))
    low_codes = low_codes.reshape(hidden_units, tp * 128)
    low_scales = jnp.moveaxis(down_scales[0].astype(F32).reshape(-1, tp, quarter), 1, 0)
    low_scales = jnp.pad(low_scales, ((0, 0), (0, 0), (0, spare)))
    parts = experts(
        rows.reshape(tp, tiles * 16, width), codes, scales, gate_up_bias.astype(F32), low_codes, low_scales
    )

    bias = jnp.pad(down_bias.astype(F32), ((0, 0), (0, spare)))
    own = lax.dynamic_slice_in_dim(hidden, col * quarter, quarter, 1)
    own = jnp.pad(own, ((0, 0), (0, spare)))
    return combine(parts.reshape(tp, tiles, 16, width), mix, bias, own, quarter, ep)


def solution(mesh):
    placed = (
        P(("groups", "ep"), None),
        P(("groups", "ep"), None),
        P(("groups", "ep"), None),
        P(),
        P("ep", None, "tp"),
        P("ep", None, "tp"),
        P("ep", "tp"),
        P("ep", "tp", None),
        P("ep", "tp", None),
        P("ep", "tp"),
    )
    return jax.shard_map(
        shards, mesh=mesh, in_specs=placed, out_specs=P(("groups", "ep"), "tp"), check_vma=False
    )
```

time: 475 us -> 228 us (0.48)
  Pallas kernels: 0 us -> 214 us
  blocking collectives: 130 us -> 0 us
  waiting for transfers between devices: 127 us -> 0 us
  local copies, waits for them, and re-layouts: 132 us -> 9.25 us
  starting transfers between devices: 29.3 us -> 0 us
  matrix products: 22.4 us -> 0 us
  other arithmetic: 18.3 us -> 4.52 us
  between operations: 13.6 us -> 0.15 us
    pallas_call x0 -> x3, Pallas kernels: none -> 214 us  [the longest x1 112 us: dispatch(): pl.pallas_call(functools.partial(dispatch_kernel, ep, tp, top, meta_at),...]
    all_to_all x1 -> x0, blocking collectives: 130 us -> none  [shards(): lax.all_to_all(own_slots, 'ep', split_axis=0, concat_axis=0, tiled=True)]
    all_to_all x2 -> x0, waiting for transfers between devices: 121 us -> none  [the longest x1 84.7 us: shards(): lax.all_to_all(answered, 'ep', split_axis=0, concat_axis=0, tiled=True)]
    slice x3 -> x0, local copies, waits for them, and re-layouts: 92.4 us -> none  [the longest x1 46.3 us: shards(): gate_part = jnp.minimum(projected[:, 0::2], 7.0)]
    all_to_all x2 -> x0, starting transfers between devices: 29.3 us -> none  [the longest x1 25.4 us: shards(): lax.all_to_all(answered, 'ep', split_axis=0, concat_axis=0, tiled=True)]
    dot_general x4 -> x0, matrix products: 22.4 us -> none  [the longest x1 9.18 us: shards(): jnp.dot(flat_rows, gate_up_weight, preferred_element_type=jnp.float32)]
    mul x2 -> x0, local copies, waits for them, and re-layouts: 12.6 us -> none  [unpack_weights(): signed_val.reshape(row_count // 32, 32, -1)]
    convert_element_type x7 -> x5, other arithmetic: 15 us -> 2.47 us  [the longest x1 1.04 us: rms_normed(): widened = hidden.astype(F32)]
  transfers between devices with their start and end apart: 3 -> 0, of which waited for: 3 -> 0; matrix products, arithmetic and copies ran while one was open for 7% -> 0% of each run, Pallas kernels for 0% -> 0%
where the time goes in v1:
time: 228 us; the launch traced here: 227 us
  Pallas kernels  214 us (94%)
  local copies, waits for them, and re-layouts  9.25 us (4%)
  other arithmetic  4.52 us (2%)
    pallas_call x1, Pallas kernels, dispatch(): pl.pallas_call(functools.partial(dispatch_kernel, ep, tp, top, meta_at),...  112 us
    pallas_call x1, Pallas kernels, combine(): pl.pallas_call(functools.partial(combine_kernel, ep, tp), out_shape=jax.S...  67.9 us
    pallas_call x1, Pallas kernels, experts(): pl.pallas_call(experts_kernel, out_shape=jax.ShapeDtypeStruct((tp, row_co...  34 us

profile of v1, /device:TPU:33, one launch (start us, length us, event | category | flops | bytes accessed | tf_op | source)
XLA Modules:
  0.0 227.5 jit_solution(12663264607402668329)
XLA Ops:
  0.0 0.8 dynamic-slice
  0.8 1.0 convert_element_type.37
  1.9 1.2 multiply_reduce_fusion
  3.1 0.1 fusion.1
  3.2 0.7 convert_element_type.40
  3.9 0.1 copy.14
  4.0 0.0 copy-done.7
  4.0 0.1 copy.15
  4.2 0.1 pad.29.clone
  4.2 0.1 maximum_maximum_fusion.block_ref
  4.3 111.6 %dispatch.1 = (bf16[4,32,16,768]{3,2,1,0:T(8,128)(2,1)S(1)}, bf16[16,128,128]{2,1,0:T(8,128)(2,1)S(1)}) custom-call(bf16[64,768]{1,0:T(8,128)(2,1)S(1)} %maximum_maximum_fusion.block_ref), custom_call_target="tpu_custom_call" | custom-call | tf_op jit(solution)/shard_map/dispatch/pallas_call | solution.py:244
  115.9 0.0 copy-start.1
  115.9 1.6 copy-done.1
  117.6 0.0 copy-done.2
  117.6 0.1 reshape_squeeze.3
  117.7 0.1 pad.20
  117.8 0.0 copy-start.4
  117.8 0.0 copy-start.3
  117.8 0.0 copy-start.5
  117.8 1.5 copy.18.low_codes_ref
  119.3 0.0 copy-done.4
  119.3 0.2 convert_element_type.45
  119.5 0.8 pad_convert_fusion.low_scales_ref
  120.3 0.0 copy-done.3
  120.3 1.0 reshape.29.scales_ref
  121.3 0.6 convert_element_type.44.bias_ref
  121.9 34.0 %experts.1 = bf16[4,512,768]{2,1,0:T(8,128)(2,1)} custom-call(bf16[4,512,768]{2,1,0:T(8,128)(2,1)} %bitcast.10, s32[360,1280]{1,0:T(8,128)} %bitcast.12, f32[45,2,1280]{2,1,0:T(2,128)} %reshape.29.scales_ref, f32[1,1280]{1,0:T(1,128)} %convert_element_type.44.bias_ref, s32[640,512]{1,0:T(8,128)} %copy.18.low_codes_ref, ...), custom_call_target="tpu_custom_call" | custom-call | tf_op jit(solution)/shard_map/experts/pallas_call | solution.py:349
  156.0 1.0 constant_dynamic-slice_fusion
  157.0 0.0 copy-done.6
  157.0 1.9 copy-done
  158.9 67.9 %combine.1 = bf16[64,720]{1,0:T(8,128)(2,1)S(1)} custom-call(bf16[4,32,16,768]{3,2,1,0:T(8,128)(2,1)S(1)} %bitcast.9, bf16[16,128,128]{2,1,0:T(8,128)(2,1)S(1)} %get-tuple-element.8.mix_ref, f32[1,768]{1,0:T(1,128)S(1)} %pad_convert_fusion.1.bias_ref, bf16[64,768]{1,0:T(8,128)(2,1)S(1)} %pad.25.own_ref), custom_call_target="tpu_custom_call" | custom-call | tf_op jit(solution)/shard_map/combine/pallas_call | solution.py:535
  226.8 0.6 copy.22
  (11 shorter events, 0.1 us)
Async XLA Ops:
  0.0 4.0 %copy-start.7 = (f32[64,4]{0,1:T(4,128)S(1)}, f32[64,4]{0,1:T(4,128)}, u32[]{:S(2)}) copy-start(f32[64,4]{0,1:T(4,128)} %param.12) | copy-start | bytes 3076
  0.0 117.6 %copy-start.2 = (s32[1,640,360]{1,2,0:T(8,128)S(1)}, s32[1,640,360]{1,2,0:T(8,128)}, u32[]{:S(2)}) copy-start(s32[1,640,360]{1,2,0:T(8,128)} %param.17) | copy-start | bytes 2764804
  115.9 1.7 copy-start.1
  117.8 1.5 copy-start.4
  117.8 2.5 %copy-start.3 = (bf16[1,90,1280]{2,1,0:T(8,128)(2,1)S(1)}, bf16[1,90,1280]{2,1,0:T(8,128)(2,1)}, u32[]{:S(2)}) copy-start(bf16[1,90,1280]{2,1,0:T(8,128)(2,1)} %param.15) | copy-start | bytes 691204
  117.8 3.5 %copy-start.5 = (bf16[1,1280]{1,0:T(2,128)(2,1)S(1)}, bf16[1,1280]{1,0:T(2,128)(2,1)}, u32[]{:S(2)}) copy-start(bf16[1,1280]{1,0:T(2,128)(2,1)} %param.16) | copy-start | bytes 7684
  121.9 35.1 %copy-start.6 = (bf16[1,720]{1,0:T(2,128)(2,1)S(1)}, bf16[1,720]{1,0:T(2,128)(2,1)}, u32[]{:S(2)}) copy-start(bf16[1,720]{1,0:T(2,128)(2,1)} %param.19) | copy-start | bytes 4324
  157.0 1.9 copy-start

commit v2 on v0

v2 whole, which is shorter than its diff:
```python
import functools

import jax
import jax.numpy as jnp
from jax import lax
from jax.experimental import pallas as pl
from jax.experimental.pallas import tpu as pltpu
from jax.sharding import PartitionSpec as P

CAP = 8
CHUNKS = 2
F32 = jnp.float32
BF16 = jnp.bfloat16


def dot(a, b):
    return jnp.dot(a, b, preferred_element_type=F32)


def iota(shape, dim):
    return lax.broadcasted_iota(jnp.int32, shape, dim)


def neighbours(ep, tp):
    me = lax.axis_index("ep")
    core = lax.rem(me, 2)
    col = lax.axis_index("tp")
    return dict(
        me=me,
        up=lax.rem(me + 2, ep),
        down=lax.rem(me + ep - 2, ep),
        pal=me + 1 - 2 * core,
        core=core,
        col=col,
        right=lax.rem(col + 1, tp),
        left=lax.rem(col + tp - 1, tp),
        across=lax.rem(col + 2, tp),
    )


def greet(at):
    barrier = pltpu.get_barrier_semaphore()
    for place in ({"ep": at["up"]}, {"ep": at["down"]}, {"ep": at["pal"]}, {"tp": at["right"]}, {"tp": at["left"]}):
        pl.semaphore_signal(barrier, inc=1, device_id=place, device_id_type=pl.DeviceIdType.MESH)
    pl.semaphore_wait(barrier, 5)


def remote(src, dst, send, recv, place):
    return pltpu.make_async_remote_copy(
        src_ref=src, dst_ref=dst, send_sem=send, recv_sem=recv, device_id=place, device_id_type=pl.DeviceIdType.MESH
    )


def nibble_value(word, shift):
    top_bits = lax.shift_left(word, 28 - shift)
    magnit = lax.shift_right_logical(top_bits, 28) & 7
    doubled = magnit + jnp.maximum(magnit - 4, 0) + 2 * jnp.maximum(magnit - 6, 0)
    value = doubled.astype(F32)
    return jnp.where(top_bits < 0, -value, value)


def layer_kernel(
    ep, tp, top, meta_at,
    block_ref, codes_hbm, scales_hbm, up_bias_ref, low_codes_hbm, low_scales_ref, down_bias_ref, own_ref,
    out_ref,
    held, handed, rows, mix,
    codes, scales, scales32, low_codes, upper, lower, spread, act, parts,
    across, summed, staged, direct, outs, given, moving, terms, own_sum,
    local_sem, zs, zr, ds, dr, xs, xr, bs, br, zs2, zr2, ds2, dr2, xs2, xr2, ts, tr, fs, fr,
):
    pairs = held.shape[0]
    tokens = held.shape[3]
    width = held.shape[4]
    part = tokens // CHUNKS
    half = pairs // 2
    columns = codes.shape[1]
    hidden_units = lower.shape[1]
    units = upper.shape[0] // tp
    word_rows = codes.shape[0]
    real_units = word_rows // 2 // tp
    words = real_units * 2
    at = neighbours(ep, tp)

    carrier = at["core"] == 1
    fetches = [
        pltpu.make_async_copy(codes_hbm, codes, local_sem.at[1]),
        pltpu.make_async_copy(scales_hbm, scales, local_sem.at[2]),
        pltpu.make_async_copy(low_codes_hbm, low_codes, local_sem.at[3]),
    ]
    for fetch in fetches:
        fetch.start()
    greet(at)

    def piece(pair, b, side, h):
        return held.at[pair, b, side, pl.ds(h * part, part)]

    def hop(s, b, side, h):
        src = piece(s - 1, b, side, h)
        if isinstance(s, int) and s == 1:
            src = piece(0, 0, 0, h) if b == 0 else block_ref.at[pl.ds(h * part, part)]
        place = {"ep": at["up"] if side == 0 else at["down"]}
        return remote(src, piece(s, b, side, h), zs.at[s, b, side, h], zr.at[s, b, side, h], place)

    def last_hop(b, side, h):
        place = {"ep": at["up"] if side == 0 else at["down"]}
        return remote(
            piece(pairs - 1, b, side, h), piece(0, b, 1, h), zs.at[0, b, side, h], zr.at[0, b, side, h], place
        )

    def last_side(h):
        return 0 if h < CHUNKS // 2 else 1

    def hand_block(pair, side):
        return remote(
            held.at[pair, 0, side], held.at[pair, 0, side], bs.at[pair, side], br.at[pair, side],
            {"ep": at["pal"]},
        )

    def lend_block():
        return remote(block_ref, held.at[0, 0, 0], bs.at[0, 0], br.at[0, 0], {"ep": at["pal"]})

    def tile(col, pos, p):
        return rows.at[col, pos * 2 + p]

    def to_pal(pos):
        return remote(handed.at[pos], tile(at["col"], pos, 1), ds.at[pos], dr.at[pos], {"ep": at["pal"]})

    def x_copy(col, pos, p, kind, place):
        return remote(
            tile(col, pos, p), tile(col, pos, p), xs.at[pos * 2 + p, kind], xr.at[pos * 2 + p, kind],
            {"tp": place},
        )

    def go_right(pos, p):
        return x_copy(at["col"], pos, p, 0, at["right"])

    def go_left(pos, p):
        return x_copy(at["col"], pos, p, 1, at["left"])

    def from_left(pos, p):
        return x_copy(at["left"], pos, p, 0, at["right"])

    def from_right(pos, p):
        return x_copy(at["right"], pos, p, 1, at["left"])

    def relay(pos, p):
        if p == 0:
            return x_copy(at["left"], pos, p, 2, at["right"])
        return x_copy(at["right"], pos, p, 2, at["left"])

    def relayed(pos, p):
        return x_copy(at["across"], pos, p, 2, at["right"])

    @pl.when(jnp.logical_not(carrier))
    def _():
        lend_block().start()

    @pl.when(carrier)
    def _():
        for h in range(CHUNKS):
            for side in range(2):
                hop(1, 1, side, h).start()
        lend_block().wait_recv()
        for h in range(CHUNKS):
            for side in range(2):
                hop(1, 0, side, h).start()
        held[0, 1, 0] = block_ref[...]

    @pl.when(jnp.logical_not(carrier))
    def _():
        held[0, 0, 0] = block_ref[...]

    both = 2 * tokens
    lane = iota((both, 128), 1)
    ls = iota((128, 128), 1)
    own_cols = (ls < 16).astype(BF16)
    pal_cols = ((ls >= 16) & (ls < 32)).astype(BF16)
    ti, tj = iota((both, both), 0), iota((both, both), 1)
    earlier = ((tj < ti) & ((ti < tokens) == (tj < tokens))).astype(BF16)
    wanted = (lax.rem(lane, 16) - jnp.where(iota((both, 128), 0) >= tokens, 8, 0)).astype(F32)
    id_lanes = (lane >= meta_at) & (lane < meta_at + top)
    own_id = at["me"].astype(F32)
    pal_id = at["pal"].astype(F32)

    def select(pair, pos):
        block = held[pair, at["core"]].reshape(both, width)
        meta = block[:, width - 128 :].astype(F32)
        weights = pltpu.roll(meta, 128 - top, axis=1)
        is_own = id_lanes & (meta == own_id)
        is_pal = id_lanes & (meta == pal_id)
        match = dot(jnp.where(is_own, 1.0, 0.0).astype(BF16), own_cols) + dot(
            jnp.where(is_pal, 1.0, 0.0).astype(BF16), pal_cols
        )
        weight = dot(jnp.where(is_own, weights, 0.0).astype(BF16), own_cols) + dot(
            jnp.where(is_pal, weights, 0.0).astype(BF16), pal_cols
        )
        slot = dot(earlier, match.astype(BF16))
        placed = (match > 0.5) & (slot == wanted)
        mix[pair] = jnp.where(placed, weight, 0.0).astype(BF16)
        pick = jnp.transpose(jnp.where(placed, 1.0, 0.0))[:32].astype(BF16)
        picked = dot(pick, block).astype(BF16)
        rows[at["col"], pos * 2] = picked[:16]
        handed[pos] = picked[16:]

    for q in range(tp):
        upper[q * units + real_units : (q + 1) * units] = jnp.zeros((units - real_units, 16, columns), BF16)
    word, lanes = iota((128, width), 0), iota((128, width), 1)
    for j in range(8):
        spread[j * 128 : (j + 1) * 128] = (lanes == 8 * word + j).astype(BF16)
    for fetch in fetches:
        fetch.wait()
    scales32[...] = 0.5 * scales[...].astype(F32)

    def decode(u):
        packed = codes[pl.ds(pl.multiple_of(u * 8, 8), 8), :]
        shift = 4 * iota((8, 8, columns), 1)
        value = nibble_value(jnp.broadcast_to(packed[:, None, :], (8, 8, columns)), shift)
        value = value.reshape(2, 32, columns)
        for k in range(2):
            scaled = (value[k] * scales32[pl.ds(2 * u + k, 1), :]).astype(BF16).reshape(2, 16, columns)
            for m in range(2):
                unit = 4 * u + 2 * k + m
                upper[unit + (units - real_units) * (unit // real_units)] = scaled[m]

    low_parts = max(1, pairs // tp)
    low_rows = hidden_units // low_parts
    low_each = tp * low_parts // pairs
    low_lanes = low_codes.shape[1]
    window = min(256, low_lanes)

    def decode_low(i):
        q, r = i // low_parts, lax.rem(i, low_parts)
        begin = jnp.minimum(128 * ((words * q) // 128), low_lanes - window)
        packed = low_codes[
            pl.ds(pl.multiple_of(r * low_rows, 32), low_rows), pl.ds(pl.multiple_of(begin, 128), window)
        ]
        packed = pltpu.roll(packed, lax.rem(window + begin - words * q, window), axis=1)[:, :128]
        whole = jnp.concatenate([nibble_value(packed, 4 * j).astype(BF16) for j in range(8)], axis=1)
        value = dot(whole, spread[...]).reshape(low_rows // 32, 32, width)
        value = value * low_scales_ref[i][:, None, :]
        lower[q, pl.ds(pl.multiple_of(r * low_rows, 32), low_rows)] = value.reshape(low_rows, width).astype(BF16)

    tiles_n = columns // 256
    si, sj = iota((256, 128), 0), iota((256, 128), 1)
    evens = (si == 2 * sj).astype(BF16)

    def project(n, part_at):
        at_n = pl.ds(pl.multiple_of(n * 256, 256), 256)
        total = jnp.broadcast_to(up_bias_ref[:, at_n], (16 * pairs, 256))
        for q in range(tp):
            weight = upper[q * units : (q + 1) * units, :, at_n].reshape(units * 16, 256)
            given_rows = rows[q, part_at * pairs : (part_at + 1) * pairs].reshape(16 * pairs, width)
            total = total + dot(given_rows, weight)
        gate = jnp.minimum(total, 7.0)
        upward = jnp.clip(pltpu.roll(total, 255, axis=1), -7.0, 7.0)
        value = (gate * jax.nn.sigmoid(1.702 * gate) * (upward + 1.0)).astype(BF16)
        act[part_at, :, pl.ds(pl.multiple_of(n * 128, 128), 128)] = dot(value, evens).astype(BF16)

    def project_down(q, part_at):
        value = dot(act[part_at], lower[q]).astype(BF16)
        parts[q, part_at * pairs : (part_at + 1) * pairs] = value.reshape(pairs, 16, width)

    lag = 2
    project_from = half + 2 * lag + 1
    projected = max(0, min(tiles_n, pairs + 2 * lag - project_from))
    decodes = word_rows // 8
    per_step = -(-decodes // min(pairs - 1, project_from))
    decode_steps = -(-decodes // per_step)

    def arrive(pos, carry):
        from_right(pos, 0).wait_recv()
        from_left(pos, 1).wait_recv()
        for p in range(2):
            relayed(pos, p).wait_recv()
        return carry

    def gather(u, carry):
        @pl.when(carrier & (u < pairs - 1))
        def _():
            s = u + 1
            for h in range(CHUNKS):
                for b in (1, 0):
                    for side in range(2):
                        hop(s, b, side, h).wait_recv()

                        @pl.when(s < pairs - 1)
                        def _():
                            hop(s + 1, b, side, h).start()

                        if side == last_side(h):

                            @pl.when(s == pairs - 1)
                            def _():
                                last_hop(b, side, h).start()

                        if b == 0 and h == CHUNKS - 1:
                            hand_block(s, side).start()

        @pl.when(carrier & (u == pairs - 1))
        def _():
            for b in range(2):
                for h in range(CHUNKS):
                    last_hop(b, last_side(h), h).wait_recv()
            hand_block(0, 1).start()

        @pl.when(u < decode_steps)
        def _():
            for k in range(per_step):
                if per_step * decode_steps == decodes:
                    decode(u * per_step + k)
                else:

                    @pl.when(u * per_step + k < decodes)
                    def _():
                        decode(u * per_step + k)

        @pl.when(jnp.logical_not(carrier) & (u < pairs - 1))
        def _():
            for side in range(2):
                hand_block(u + 1, side).wait_recv()

        @pl.when(jnp.logical_not(carrier) & (u == pairs - 1))
        def _():
            hand_block(0, 1).wait_recv()

        @pl.when(u < pairs)
        def _():
            select(lax.rem(u + 1, pairs), u)
            to_pal(u).start()
            go_right(u, 0).start()
            go_left(u, 0).start()

        @pl.when((u >= lag) & (u < pairs + lag))
        def _():
            to_pal(u - lag).wait_recv()
            go_right(u - lag, 1).start()
            go_left(u - lag, 1).start()
            from_left(u - lag, 0).wait_recv()
            relay(u - lag, 0).start()

        @pl.when(u >= 2 * lag)
        def _():
            from_right(u - 2 * lag, 1).wait_recv()
            relay(u - 2 * lag, 1).start()

        @pl.when(u < pairs)
        def _():
            for k in range(low_each):
                decode_low(u * low_each + k)

        if projected:

            @pl.when(u == project_from)
            def _():
                lax.fori_loop(0, half, arrive, 0)

            @pl.when((u >= project_from) & (u < project_from + projected))
            def _():
                project(u - project_from, 0)

        return carry

    lax.fori_loop(0, pairs + 2 * lag, gather, 0)
    lax.fori_loop(half if projected else 0, pairs, arrive, 0)

    def project_rest(n, carry):
        project(n, 0)
        return carry

    def project_late(n, carry):
        project(n, 1)
        return carry

    def down_late(q, carry):
        project_down(q, 1)
        return carry

    if projected < tiles_n:
        lax.fori_loop(projected, tiles_n, project_rest, 0)
    lax.fori_loop(0, tiles_n, project_late, 0)
    lax.fori_loop(0, tp, down_late, 0)

    def out_side(h):
        return 1 if h < CHUNKS // 2 else 0

    def up_or_down(side):
        return {"ep": at["up"] if side == 1 else at["down"]}

    def sum_hop(s, b, side, h):
        src = moving.at[s, b, side, pl.ds(h * part, part)]
        dst = moving.at[s - 1, b, side, pl.ds(h * part, part)]
        return remote(src, dst, zs2.at[s - 1, b, side, h], zr2.at[s - 1, b, side, h], up_or_down(side))

    def first_sum(b, side, h):
        src = terms.at[0, b, 1, pl.ds(h * part, part)]
        dst = moving.at[pairs - 1, b, side, pl.ds(h * part, part)]
        return remote(
            src, dst, zs2.at[pairs - 1, b, side, h], zr2.at[pairs - 1, b, side, h], up_or_down(side)
        )

    def lend_terms(pair):
        return remote(terms.at[pair, 0], terms.at[pair, 0], ts.at[pair], tr.at[pair], {"ep": at["pal"]})

    def hand_sum(side):
        return remote(moving.at[0, 0, side], moving.at[0, 0, side], fs.at[side], fr.at[side], {"ep": at["pal"]})

    def far(p):
        return {"tp": at["right"] if p == 0 else at["left"]}

    def near(p):
        return {"tp": at["left"] if p == 0 else at["right"]}

    def two_away(t, p):
        return remote(parts.at[at["across"], t], across.at[t], xs2.at[t, 0], xr2.at[t, 0], far(p))

    def one_away(t, p):
        col = at["left"] if p == 0 else at["right"]
        return remote(parts.at[col, t], direct.at[t], xs2.at[t, 1], xr2.at[t, 1], near(p))

    def onward(t, p):
        return remote(staged.at[t], summed.at[t], xs2.at[t, 2], xr2.at[t, 2], far(p))

    def give(pos):
        return remote(given.at[pos], outs.at[pos, pl.ds(16, 16)], ds2.at[pos], dr2.at[pos], {"ep": at["pal"]})

    for h in range(CHUNKS):
        side = 1 - out_side(h)
        for b in range(2):
            moving[pairs - 1, b, side, h * part : (h + 1) * part] = jnp.zeros((part, width), BF16)

    down_each = -(-tp // (half - 1)) if half > 1 else tp

    if half <= 1:
        for q in range(tp):
            project_down(q, 0)

    def scatter(t, carry):
        @pl.when(t < pairs)
        def _():
            pos = pairs - 1 - t
            for p in range(2):
                two_away(pos * 2 + p, p).start()
            for p in range(2):
                one_away(pos * 2 + p, p).start()

        @pl.when(carrier & (t >= 8))
        def _():
            u = t - 8
            pair = lax.rem(pairs - u, pairs)
            lend_terms(pair).wait_recv()

            @pl.when(u == 0)
            def _():
                for h in range(CHUNKS):
                    for b in range(2):
                        first_sum(b, out_side(h), h).start()

            @pl.when(u > 0)
            def _():
                for h in range(CHUNKS):
                    for b in (1, 0):
                        for side in (out_side(h), 1 - out_side(h)):
                            rows_at = pl.ds(h * part, part)
                            arrival = remote(
                                moving.at[pair, b, side, rows_at],
                                moving.at[pair, b, side, rows_at],
                                zs2.at[pair, b, side, h],
                                zr2.at[pair, b, side, h],
                                up_or_down(side),
                            )
                            if side == out_side(h):
                                arrival.wait_recv()
                            else:

                                @pl.when(u > 1)
                                def _():
                                    arrival.wait_recv()

                            value = moving[pair, b, side, rows_at].astype(F32) + terms[
                                pair, b, side, rows_at
                            ].astype(F32)
                            moving[pair, b, side, rows_at] = value.astype(BF16)
                            sum_hop(pair, b, side, h).start()

        @pl.when((t >= 6) & (t < pairs + 6))
        def _():
            pos = pairs + 5 - t
            pair = lax.rem(pos + 1, pairs)
            give(pos).wait_recv()
            mixed = dot(mix[pair][:, :32], outs[pos])
            terms[pair, at["core"]] = mixed.astype(BF16).reshape(2, tokens, width)

            @pl.when(t == 6)
            def _():
                own_sum[...] = mixed[:tokens]

            @pl.when(jnp.logical_not(carrier))
            def _():
                lend_terms(pair).start()

        @pl.when((t >= 2) & (t < pairs + 2))
        def _():
            for p in range(2):
                t1 = (pairs + 1 - t) * 2 + p
                two_away(t1, p).wait_recv()
                col = at["right"] if p == 0 else at["left"]
                staged[t1] = (across[t1].astype(F32) + parts[col, t1].astype(F32)).astype(BF16)
                onward(t1, p).start()

        @pl.when((t >= 4) & (t < pairs + 4))
        def _():
            pos = pairs + 3 - t
            for p in (1, 0):
                t2 = pos * 2 + p
                one_away(t2, p).wait_recv()
                onward(t2, p).wait_recv()
                total = (
                    summed[t2].astype(F32)
                    + direct[t2].astype(F32)
                    + parts[at["col"], t2].astype(F32)
                    + down_bias_ref[...]
                ).astype(BF16)
                if p == 1:
                    given[pos] = total
                    give(pos).start()
                else:
                    outs[pos, :16] = total

        if half > 1:
            for k in range(down_each):
                q = (t - 1) * down_each + k

                @pl.when((t >= 1) & (q < tp))
                def _():
                    project_down(q, 0)

        return carry

    lax.fori_loop(0, pairs + 8, scatter, 0)

    @pl.when(carrier)
    def _():
        for b in range(2):
            for side in range(2):
                for h in range(CHUNKS):
                    sum_hop(1, b, side, h).wait_recv()
                if b == 0:
                    hand_sum(side).start()

    @pl.when(jnp.logical_not(carrier))
    def _():
        for side in range(2):
            hand_sum(side).wait_recv()

    core = at["core"]
    total = own_ref[...].astype(F32) + own_sum[...]
    total = total + moving[0, core, 0].astype(F32) + moving[0, core, 1].astype(F32)
    out_ref[...] = total[:, : out_ref.shape[1]].astype(BF16)

    def finish(pos, carry):
        to_pal(pos).wait_send()
        give(pos).wait_send()
        for p in range(2):
            go_right(pos, p).wait_send()
            go_left(pos, p).wait_send()
            relay(pos, p).wait_send()
            two_away(pos * 2 + p, p).wait_send()
            one_away(pos * 2 + p, p).wait_send()
            onward(pos * 2 + p, p).wait_send()
        return carry

    lax.fori_loop(0, pairs, finish, 0)

    @pl.when(carrier)
    def _():
        def sent(s, carry):
            for b in range(2):
                for side in range(2):
                    for h in range(CHUNKS):
                        hop(s, b, side, h).wait_send()
                        sum_hop(s, b, side, h).wait_send()
            for side in range(2):
                hand_block(s, side).wait_send()
            return carry

        lax.fori_loop(1, pairs, sent, 0)
        hand_block(0, 1).wait_send()
        for b in range(2):
            for h in range(CHUNKS):
                last_hop(b, last_side(h), h).wait_send()
                first_sum(b, out_side(h), h).wait_send()
        for side in range(2):
            hand_sum(side).wait_send()

    @pl.when(jnp.logical_not(carrier))
    def _():
        lend_block().wait_send()

        def lent(pair, carry):
            lend_terms(pair).wait_send()
            return carry

        lax.fori_loop(0, pairs, lent, 0)


def layer(block, codes, scales, up_bias, low_codes, low_scales, down_bias, own, quarter, ep, tp, top):
    tokens, width = block.shape
    pairs = ep // 4
    word_rows, columns = codes.shape
    hidden_units, low_lanes = low_codes.shape
    tiles = 2 * pairs
    dma = pltpu.SemaphoreType.DMA
    vmem = pl.BlockSpec(memory_space=pltpu.VMEM)
    hbm = pl.BlockSpec(memory_space=pl.ANY)
    ring = dma((pairs, 2, 2, CHUNKS))
    return pl.pallas_call(
        functools.partial(layer_kernel, ep, tp, top, quarter - (width - 128)),
        out_shape=jax.ShapeDtypeStruct((tokens, quarter), BF16),
        in_specs=[vmem, hbm, hbm, vmem, hbm, vmem, vmem, vmem],
        out_specs=vmem,
        scratch_shapes=[
            pltpu.VMEM((pairs, 2, 2, tokens, width), BF16),
            pltpu.VMEM((pairs, 16, width), BF16),
            pltpu.VMEM((tp, tiles, 16, width), BF16),
            pltpu.VMEM((pairs, 2 * tokens, 128), BF16),
            pltpu.VMEM((word_rows, columns), jnp.int32),
            pltpu.VMEM(scales.shape, BF16),
            pltpu.VMEM(scales.shape, F32),
            pltpu.VMEM((hidden_units, low_lanes), jnp.int32),
            pltpu.VMEM((tp * width // 16, 16, columns), BF16),
            pltpu.VMEM((tp, hidden_units, width), BF16),
            pltpu.VMEM((1024, width), BF16),
            pltpu.VMEM((2, 16 * pairs, hidden_units), BF16),
            pltpu.VMEM((tp, tiles, 16, width), BF16),
            pltpu.VMEM((tiles, 16, width), BF16),
            pltpu.VMEM((tiles, 16, width), BF16),
            pltpu.VMEM((tiles, 16, width), BF16),
            pltpu.VMEM((tiles, 16, width), BF16),
            pltpu.VMEM((pairs, 32, width), BF16),
            pltpu.VMEM((pairs, 16, width), BF16),
            pltpu.VMEM((pairs, 2, 2, tokens, width), BF16),
            pltpu.VMEM((pairs, 2, 2, tokens, width), BF16),
            pltpu.VMEM((tokens, width), F32),
            dma((4,)),
            ring, ring, dma((pairs,)), dma((pairs,)), dma((tiles, 3)), dma((tiles, 3)),
            dma((pairs, 2)), dma((pairs, 2)),
            ring, ring, dma((pairs,)), dma((pairs,)), dma((tiles, 3)), dma((tiles, 3)),
            dma((pairs,)), dma((pairs,)), dma((2,)), dma((2,)),
        ],
        compiler_params=pltpu.CompilerParams(
            collective_id=0, has_side_effects=True, vmem_limit_bytes=60 << 20
        ),
        name="layer",
    )(block, codes, scales, up_bias, low_codes, low_scales, down_bias, own)


def rms_normed(hidden, norm_gain):
    widened = hidden.astype(F32)
    mean_square = jnp.mean(widened * widened, axis=-1, keepdims=True)
    scaled = widened * lax.rsqrt(mean_square + 1e-05) * norm_gain.astype(F32)
    return scaled.astype(BF16)


def shards(
    hidden,
    route_experts,
    route_weight,
    norm_gain,
    gate_up_codes,
    gate_up_scales,
    gate_up_bias,
    down_codes,
    down_scales,
    down_bias,
):
    ep = lax.axis_size("ep")
    tp = lax.axis_size("tp")
    col = lax.axis_index("tp")
    tokens, model_width = hidden.shape
    top = route_experts.shape[1]
    quarter = model_width // tp
    width = -(-(quarter + 2 * top) // 128) * 128
    spare = width - quarter
    normed = rms_normed(hidden, norm_gain)
    own_normed = lax.dynamic_slice_in_dim(normed, col * quarter, quarter, 1)
    block = jnp.concatenate(
        [
            own_normed,
            route_experts.astype(BF16),
            route_weight.astype(BF16),
            jnp.zeros((tokens, spare - 2 * top), BF16),
        ],
        axis=1,
    )
    hidden_units = down_codes.shape[1]
    low_codes = jnp.pad(down_codes[0], ((0, 0), (0, -(down_codes.shape[2]) % 128)))
    low_parts = max(1, ep // 4 // tp)
    low_scales = 0.5 * down_scales[0].astype(F32).reshape(-1, tp, quarter)
    low_scales = jnp.pad(jnp.moveaxis(low_scales, 1, 0), ((0, 0), (0, 0), (0, spare)))
    low_scales = low_scales.reshape(tp * low_parts, hidden_units // 32 // low_parts, width)
    bias = jnp.pad(down_bias.astype(F32), ((0, 0), (0, spare)))
    own = lax.dynamic_slice_in_dim(hidden, col * quarter, quarter, 1)
    own = jnp.pad(own, ((0, 0), (0, spare)))
    return layer(
        block, gate_up_codes[0], gate_up_scales[0], gate_up_bias.astype(F32), low_codes, low_scales, bias, own,
        quarter, ep, tp, top,
    )


def solution(mesh):
    placed = (
        P(("groups", "ep"), None),
        P(("groups", "ep"), None),
        P(("groups", "ep"), None),
        P(),
        P("ep", None, "tp"),
        P("ep", None, "tp"),
        P("ep", "tp"),
        P("ep", "tp", None),
        P("ep", "tp", None),
        P("ep", "tp"),
    )
    return jax.shard_map(
        shards, mesh=mesh, in_specs=placed, out_specs=P(("groups", "ep"), "tp"), check_vma=False
    )
```

time: 475 us -> 198 us (0.42)
  Pallas kernels: 0 us -> 185 us
  blocking collectives: 130 us -> 0 us
  waiting for transfers between devices: 127 us -> 0 us
  local copies, waits for them, and re-layouts: 132 us -> 6.7 us
  starting transfers between devices: 29.3 us -> 0 us
  matrix products: 22.4 us -> 0 us
  between operations: 13.6 us -> 0.09 us
  other arithmetic: 18.3 us -> 5.74 us
    pallas_call x0 -> x1, Pallas kernels: none -> 185 us  [layer(): pl.pallas_call(functools.partial(layer_kernel, ep, tp, top, quarter - (wi...]
    all_to_all x1 -> x0, blocking collectives: 130 us -> none  [shards(): lax.all_to_all(own_slots, 'ep', split_axis=0, concat_axis=0, tiled=True)]
    all_to_all x2 -> x0, waiting for transfers between devices: 121 us -> none  [the longest x1 84.7 us: shards(): lax.all_to_all(answered, 'ep', split_axis=0, concat_axis=0, tiled=True)]
    slice x3 -> x0, local copies, waits for them, and re-layouts: 92.4 us -> none  [the longest x1 46.3 us: shards(): gate_part = jnp.minimum(projected[:, 0::2], 7.0)]
    all_to_all x2 -> x0, starting transfers between devices: 29.3 us -> none  [the longest x1 25.4 us: shards(): lax.all_to_all(answered, 'ep', split_axis=0, concat_axis=0, tiled=True)]
    dot_general x4 -> x0, matrix products: 22.4 us -> none  [the longest x1 9.18 us: shards(): jnp.dot(flat_rows, gate_up_weight, preferred_element_type=jnp.float32)]
    convert_element_type x3 -> x2, local copies, waits for them, and re-layouts: 13.5 us -> 0.23 us  [the longest x1 0.11 us: shards(): route_weight.astype(BF16)]
    mul x2, local copies, waits for them, and re-layouts: 12.6 us -> 0.26 us  [shards(): low_scales = 0.5 * down_scales[0].astype(F32).reshape(-1, tp, quarter)]
  transfers between devices with their start and end apart: 3 -> 0, of which waited for: 3 -> 0; matrix products, arithmetic and copies ran while one was open for 7% -> 0% of each run, Pallas kernels for 0% -> 0%
where the time goes in v2:
time: 198 us
  Pallas kernels  185 us (93%)
  local copies, waits for them, and re-layouts  6.7 us (3%)
  other arithmetic  5.74 us (3%)
    pallas_call x1, Pallas kernels, layer(): pl.pallas_call(functools.partial(layer_kernel, ep, tp, top, quarter - (wi...  185 us

profile of v2, /device:TPU:33, one launch (start us, length us, event | category | flops | bytes accessed | tf_op | source)
XLA Modules:
  0.0 197.5 jit_solution(1723587393047522581)
XLA Ops:
  0.0 0.0 copy-start.2
  0.0 0.0 copy-start
  0.0 0.8 convert_element_type.34
  0.8 0.1 copy.16
  0.9 0.7 convert_element_type.33
  1.6 0.1 copy.15
  1.7 1.0 convert_element_type.30
  2.7 0.8 dynamic-slice
  3.5 1.2 multiply_reduce_fusion
  4.7 0.1 fusion.1
  4.8 0.1 pad.26.clone
  4.9 0.7 maximum_maximum_fusion.block_ref
  5.6 0.0 copy-done.2
  5.7 0.6 convert_element_type.35.up_bias_ref
  6.2 0.0 copy-done
  6.2 0.0 copy-start.1
  6.2 0.3 copy.17
  6.6 1.0 pad.18.low_codes_hbm
  7.6 0.0 copy-done.1
  7.6 0.0 copy-start.3
  7.6 0.2 mul.40
  7.9 0.8 reshape.17.low_scales_ref
  8.7 0.0 copy-done.3
  8.7 0.6 pad_convert_fusion.down_bias_ref
  9.3 1.0 constant_dynamic-slice_fusion
  10.3 0.6 pad.22.own_ref
  11.0 185.0 %layer.1 = bf16[64,720]{1,0:T(8,128)(2,1)} custom-call(bf16[64,768]{1,0:T(8,128)(2,1)} %maximum_maximum_fusion.block_ref, s32[360,1280]{1,0:T(8,128)} %bitcast.7, bf16[90,1280]{1,0:T(8,128)(2,1)} %bitcast.9, f32[1,1280]{1,0:T(1,128)} %convert_element_type.35.up_bias_ref, s32[640,384]{1,0:T(8,128)} %pad.18.low_codes_hbm, ...), custom_call_target="tpu_custom_call" | custom-call | tf_op jit(solution)/shard_map/layer/pallas_call | solution.py:616
  196.0 1.5 copy.22
  (5 shorter events, 0.1 us)
Async XLA Ops:
  0.0 5.6 %copy-start.2 = (bf16[1,1280]{1,0:T(2,128)(2,1)S(1)}, bf16[1,1280]{1,0:T(2,128)(2,1)}, u32[]{:S(2)}) copy-start(bf16[1,1280]{1,0:T(2,128)(2,1)} %param.16) | copy-start | bytes 7684
  0.0 6.2 %copy-start = (s32[1,640,360]{1,2,0:T(8,128)S(1)}, s32[1,640,360]{1,2,0:T(8,128)}, u32[]{:S(2)}) copy-start(s32[1,640,360]{1,2,0:T(8,128)} %param.17) | copy-start | bytes 2764804
  6.2 1.4 copy-start.1
  7.6 1.1 copy-start.3

commit v3 on v2

--- a/solution.py
+++ b/solution.py
@@ -8,7 +8,7 @@
 from jax.sharding import PartitionSpec as P
 
 CAP = 8
-CHUNKS = 2
+CHUNKS = 4
 F32 = jnp.float32
 BF16 = jnp.bfloat16
 
@@ -27,10 +27,9 @@
     col = lax.axis_index("tp")
     return dict(
         me=me,
-        up=lax.rem(me + 2, ep),
-        down=lax.rem(me + ep - 2, ep),
+        up=lax.rem(me + 3 - 2 * core, ep),
+        down=lax.rem(me + ep - 1 - 2 * core, ep),
         pal=me + 1 - 2 * core,
-        core=core,
         col=col,
         right=lax.rem(col + 1, tp),
         left=lax.rem(col + tp - 1, tp),
@@ -61,16 +60,17 @@
 
 def layer_kernel(
     ep, tp, top, meta_at,
-    block_ref, codes_hbm, scales_hbm, up_bias_ref, low_codes_hbm, low_scales_ref, down_bias_ref, own_ref,
+    hidden_ref, ids_ref, weights_ref, gain_ref, codes_hbm, scales_hbm, up_bias_ref, low_codes_hbm,
+    low_scales_hbm, down_bias_ref,
     out_ref,
-    held, handed, rows, mix,
+    turned_codes,    wide, wide_scales, narrow_scales, low_scales, down_bias, own, block_ref, held, handed, rows, mix,
     codes, scales, scales32, low_codes, upper, lower, spread, act, parts,
     across, summed, staged, direct, outs, given, moving, terms, own_sum,
-    local_sem, zs, zr, ds, dr, xs, xr, bs, br, zs2, zr2, ds2, dr2, xs2, xr2, ts, tr, fs, fr,
+    local_sem, zs, zr, ds, dr, xs, xr, zs2, zr2, ds2, dr2, xs2, xr2,
 ):
     pairs = held.shape[0]
-    tokens = held.shape[3]
-    width = held.shape[4]
+    tokens = held.shape[2]
+    width = held.shape[3]
     part = tokens // CHUNKS
     half = pairs // 2
     columns = codes.shape[1]
@@ -81,43 +81,57 @@
     words = real_units * 2
     at = neighbours(ep, tp)
 
-    carrier = at["core"] == 1
     fetches = [
         pltpu.make_async_copy(codes_hbm, codes, local_sem.at[1]),
         pltpu.make_async_copy(scales_hbm, scales, local_sem.at[2]),
-        pltpu.make_async_copy(low_codes_hbm, low_codes, local_sem.at[3]),
+        pltpu.make_async_copy(low_codes_hbm, turned_codes.at[pl.ds(0, low_codes_hbm.shape[0])], local_sem.at[3]),
+        pltpu.make_async_copy(low_scales_hbm, narrow_scales, local_sem.at[0]),
     ]
     for fetch in fetches:
         fetch.start()
+
+    model_width = hidden_ref.shape[1]
+    quarter = out_ref.shape[1]
+    whole_width = wide.shape[1]
+    rest = jnp.zeros((tokens, whole_width - model_width), F32)
+    widened = hidden_ref[...].astype(F32)
+    mean_square = jnp.mean(widened * widened, axis=-1, keepdims=True)
+    back = lax.rem(whole_width - at["col"] * quarter, whole_width)
+    wide[:, :model_width] = widened
+    wide[:, model_width:] = rest
+    own[...] = pltpu.roll(wide[...], back, axis=1)[:, :width]
+    wide[:8, :model_width] = jnp.broadcast_to(gain_ref[...].astype(F32), (8, model_width))
+    gain = pltpu.roll(wide[:8], back, axis=1)[:1, :width]
+    normed = (own[...] * lax.rsqrt(mean_square + 1e-05) * gain).astype(BF16).astype(F32)
+    choice, meta_lane = iota((top, 128), 0), iota((top, 128), 1)
+    meta_own = dot(ids_ref[...].astype(F32).astype(BF16), (meta_lane == meta_at + choice).astype(BF16))
+    meta_own = meta_own + dot(
+        weights_ref[...].astype(BF16), (meta_lane == meta_at + top + choice).astype(BF16)
+    )
+    if width > 128:
+        block_ref[:, : width - 128] = normed[:, : width - 128].astype(BF16)
+    is_data = iota((tokens, 128), 1) < meta_at
+    block_ref[:, width - 128 :] = jnp.where(is_data, normed[:, width - 128 :], meta_own).astype(BF16)
     greet(at)
 
-    def piece(pair, b, side, h):
-        return held.at[pair, b, side, pl.ds(h * part, part)]
-
-    def hop(s, b, side, h):
-        src = piece(s - 1, b, side, h)
+    def piece(pair, side, h):
+        return held.at[pair, side, pl.ds(h * part, part)]
+
+    def hop(s, side, h):
+        src = piece(s - 1, side, h)
         if isinstance(s, int) and s == 1:
-            src = piece(0, 0, 0, h) if b == 0 else block_ref.at[pl.ds(h * part, part)]
+            src = block_ref.at[pl.ds(h * part, part)]
         place = {"ep": at["up"] if side == 0 else at["down"]}
-        return remote(src, piece(s, b, side, h), zs.at[s, b, side, h], zr.at[s, b, side, h], place)
-
-    def last_hop(b, side, h):
+        return remote(src, piece(s, side, h), zs.at[s, side, h], zr.at[s, side, h], place)
+
+    def last_hop(side, h):
         place = {"ep": at["up"] if side == 0 else at["down"]}
         return remote(
-            piece(pairs - 1, b, side, h), piece(0, b, 1, h), zs.at[0, b, side, h], zr.at[0, b, side, h], place
+            piece(pairs - 1, side, h), piece(0, 1, h), zs.at[0, side, h], zr.at[0, side, h], place
         )
 
     def last_side(h):
         return 0 if h < CHUNKS // 2 else 1
-
-    def hand_block(pair, side):
-        return remote(
-            held.at[pair, 0, side], held.at[pair, 0, side], bs.at[pair, side], br.at[pair, side],
-            {"ep": at["pal"]},
-        )
-
-    def lend_block():
-        return remote(block_ref, held.at[0, 0, 0], bs.at[0, 0], br.at[0, 0], {"ep": at["pal"]})
 
     def tile(col, pos, p):
         return rows.at[col, pos * 2 + p]
@@ -151,24 +165,10 @@
     def relayed(pos, p):
         return x_copy(at["across"], pos, p, 2, at["right"])
 
-    @pl.when(jnp.logical_not(carrier))
-    def _():
-        lend_block().start()
-
-    @pl.when(carrier)
-    def _():
-        for h in range(CHUNKS):
-            for side in range(2):
-                hop(1, 1, side, h).start()
-        lend_block().wait_recv()
-        for h in range(CHUNKS):
-            for side in range(2):
-                hop(1, 0, side, h).start()
-        held[0, 1, 0] = block_ref[...]
-
-    @pl.when(jnp.logical_not(carrier))
-    def _():
-        held[0, 0, 0] = block_ref[...]
+    for h in range(CHUNKS):
+        for side in range(2):
+            hop(1, side, h).start()
+    held[0, 0] = block_ref[...]
 
     both = 2 * tokens
     lane = iota((both, 128), 1)
@@ -183,7 +183,7 @@
     pal_id = at["pal"].astype(F32)
 
     def select(pair, pos):
-        block = held[pair, at["core"]].reshape(both, width)
+        block = held[pair].reshape(both, width)
         meta = block[:, width - 128 :].astype(F32)
         weights = pltpu.roll(meta, 128 - top, axis=1)
         is_own = id_lanes & (meta == own_id)
@@ -209,7 +209,23 @@
         spread[j * 128 : (j + 1) * 128] = (lanes == 8 * word + j).astype(BF16)
     for fetch in fetches:
         fetch.wait()
+    turned_codes[words * tp :] = jnp.zeros((turned_codes.shape[0] - words * tp, hidden_units), jnp.int32)
+    low_codes[...] = jnp.transpose(turned_codes[...])
     scales32[...] = 0.5 * scales[...].astype(F32)
+    low_parts = max(1, pairs // tp)
+    blocks = wide_scales.shape[0]
+    each = blocks // low_parts
+    wide_scales[:, :model_width] = 0.5 * narrow_scales[...].astype(F32)
+    wide_scales[:, model_width:] = jnp.zeros((blocks, whole_width - model_width), F32)
+    for q in range(tp):
+        turned = wide_scales[...]
+        if q:
+            turned = pltpu.roll(turned, whole_width - q * quarter, axis=1)
+        turned = jnp.where(iota((blocks, width), 1) < quarter, turned[:, :width], 0.0)
+        for r in range(low_parts):
+            low_scales[q * low_parts + r] = turned[r * each : (r + 1) * each]
+    down_bias[...] = jnp.zeros_like(down_bias)
+    down_bias[:, :quarter] = down_bias_ref[...].astype(F32)
 
     def decode(u):
         packed = codes[pl.ds(pl.multiple_of(u * 8, 8), 8), :]
@@ -222,7 +238,6 @@
                 unit = 4 * u + 2 * k + m
                 upper[unit + (units - real_units) * (unit // real_units)] = scaled[m]
 
-    low_parts = max(1, pairs // tp)
     low_rows = hidden_units // low_parts
     low_each = tp * low_parts // pairs
     low_lanes = low_codes.shape[1]
@@ -237,7 +252,7 @@
         packed = pltpu.roll(packed, lax.rem(window + begin - words * q, window), axis=1)[:, :128]
         whole = jnp.concatenate([nibble_value(packed, 4 * j).astype(BF16) for j in range(8)], axis=1)
         value = dot(whole, spread[...]).reshape(low_rows // 32, 32, width)
-        value = value * low_scales_ref[i][:, None, :]
+        value = value * low_scales[i][:, None, :]
         lower[q, pl.ds(pl.multiple_of(r * low_rows, 32), low_rows)] = value.reshape(low_rows, width).astype(BF16)
 
     tiles_n = columns // 256
@@ -246,7 +261,7 @@
 
     def project(n, part_at):
         at_n = pl.ds(pl.multiple_of(n * 256, 256), 256)
-        total = jnp.broadcast_to(up_bias_ref[:, at_n], (16 * pairs, 256))
+        total = jnp.broadcast_to(up_bias_ref[:, at_n].astype(F32), (16 * pairs, 256))
         for q in range(tp):
             weight = upper[q * units : (q + 1) * units, :, at_n].reshape(units * 16, 256)
             given_rows = rows[q, part_at * pairs : (part_at + 1) * pairs].reshape(16 * pairs, width)
@@ -275,33 +290,27 @@
         return carry
 
     def gather(u, carry):
-        @pl.when(carrier & (u < pairs - 1))
+        @pl.when(u < pairs - 1)
         def _():
             s = u + 1
             for h in range(CHUNKS):
-                for b in (1, 0):
-                    for side in range(2):
-                        hop(s, b, side, h).wait_recv()
-
-                        @pl.when(s < pairs - 1)
+                for side in range(2):
+                    hop(s, side, h).wait_recv()
+
+                    @pl.when(s < pairs - 1)
+                    def _():
+                        hop(s + 1, side, h).start()
+
+                    if side == last_side(h):
+
+                        @pl.when(s == pairs - 1)
                         def _():
-                            hop(s + 1, b, side, h).start()
-
-                        if side == last_side(h):
-
-                            @pl.when(s == pairs - 1)
-                            def _():
-                                last_hop(b, side, h).start()
-
-                        if b == 0 and h == CHUNKS - 1:
-                            hand_block(s, side).start()
-
-        @pl.when(carrier & (u == pairs - 1))
-        def _():
-            for b in range(2):
-                for h in range(CHUNKS):
-                    last_hop(b, last_side(h), h).wait_recv()
-            hand_block(0, 1).start()
+                            last_hop(side, h).start()
+
+        @pl.when(u == pairs - 1)
+        def _():
+            for h in range(CHUNKS):
+                last_hop(last_side(h), h).wait_recv()
 
         @pl.when(u < decode_steps)
         def _():
@@ -313,15 +322,6 @@
                     @pl.when(u * per_step + k < decodes)
                     def _():
                         decode(u * per_step + k)
-
-        @pl.when(jnp.logical_not(carrier) & (u < pairs - 1))
-        def _():
-            for side in range(2):
-                hand_block(u + 1, side).wait_recv()
-
-        @pl.when(jnp.logical_not(carrier) & (u == pairs - 1))
-        def _():
-            hand_block(0, 1).wait_recv()
 
         @pl.when(u < pairs)
         def _():
@@ -386,23 +386,15 @@
     def up_or_down(side):
         return {"ep": at["up"] if side == 1 else at["down"]}
 
-    def sum_hop(s, b, side, h):
-        src = moving.at[s, b, side, pl.ds(h * part, part)]
-        dst = moving.at[s - 1, b, side, pl.ds(h * part, part)]
-        return remote(src, dst, zs2.at[s - 1, b, side, h], zr2.at[s - 1, b, side, h], up_or_down(side))
-
-    def first_sum(b, side, h):
-        src = terms.at[0, b, 1, pl.ds(h * part, part)]
-        dst = moving.at[pairs - 1, b, side, pl.ds(h * part, part)]
-        return remote(
-            src, dst, zs2.at[pairs - 1, b, side, h], zr2.at[pairs - 1, b, side, h], up_or_down(side)
-        )
-
-    def lend_terms(pair):
-        return remote(terms.at[pair, 0], terms.at[pair, 0], ts.at[pair], tr.at[pair], {"ep": at["pal"]})
-
-    def hand_sum(side):
-        return remote(moving.at[0, 0, side], moving.at[0, 0, side], fs.at[side], fr.at[side], {"ep": at["pal"]})
+    def sum_hop(s, side, h):
+        src = moving.at[s, side, pl.ds(h * part, part)]
+        dst = moving.at[s - 1, side, pl.ds(h * part, part)]
+        return remote(src, dst, zs2.at[s - 1, side, h], zr2.at[s - 1, side, h], up_or_down(side))
+
+    def first_sum(side, h):
+        src = terms.at[0, 1, pl.ds(h * part, part)]
+        dst = moving.at[pairs - 1, side, pl.ds(h * part, part)]
+        return remote(src, dst, zs2.at[pairs - 1, side, h], zr2.at[pairs - 1, side, h], up_or_down(side))
 
     def far(p):
         return {"tp": at["right"] if p == 0 else at["left"]}
@@ -425,8 +417,7 @@
 
     for h in range(CHUNKS):
         side = 1 - out_side(h)
-        for b in range(2):
-            moving[pairs - 1, b, side, h * part : (h + 1) * part] = jnp.zeros((part, width), BF16)
+        moving[pairs - 1, side, h * part : (h + 1) * part] = jnp.zeros((part, width), BF16)
 
     down_each = -(-tp // (half - 1)) if half > 1 else tp
 
@@ -443,44 +434,39 @@
             for p in range(2):
                 one_away(pos * 2 + p, p).start()
 
-        @pl.when(carrier & (t >= 8))
-        def _():
-            u = t - 8
+        @pl.when(t >= 7)
+        def _():
+            u = t - 7
             pair = lax.rem(pairs - u, pairs)
-            lend_terms(pair).wait_recv()
 
             @pl.when(u == 0)
             def _():
                 for h in range(CHUNKS):
-                    for b in range(2):
-                        first_sum(b, out_side(h), h).start()
+                    first_sum(out_side(h), h).start()
 
             @pl.when(u > 0)
             def _():
                 for h in range(CHUNKS):
-                    for b in (1, 0):
-                        for side in (out_side(h), 1 - out_side(h)):
-                            rows_at = pl.ds(h * part, part)
-                            arrival = remote(
-                                moving.at[pair, b, side, rows_at],
-                                moving.at[pair, b, side, rows_at],
-                                zs2.at[pair, b, side, h],
-                                zr2.at[pair, b, side, h],
-                                up_or_down(side),
-                            )
-                            if side == out_side(h):
+                    for side in (out_side(h), 1 - out_side(h)):
+                        rows_at = pl.ds(h * part, part)
+                        arrival = remote(
+                            moving.at[pair, side, rows_at],
+                            moving.at[pair, side, rows_at],
+                            zs2.at[pair, side, h],
+                            zr2.at[pair, side, h],
+                            up_or_down(side),
+                        )
+                        if side == out_side(h):
+                            arrival.wait_recv()
+                        else:
+
+                            @pl.when(u > 1)
+                            def _():
                                 arrival.wait_recv()
-                            else:
-
-                                @pl.when(u > 1)
-                                def _():
-                                    arrival.wait_recv()
-
-                            value = moving[pair, b, side, rows_at].astype(F32) + terms[
-                                pair, b, side, rows_at
-                            ].astype(F32)
-                            moving[pair, b, side, rows_at] = value.astype(BF16)
-                            sum_hop(pair, b, side, h).start()
+
+                        value = moving[pair, side, rows_at].astype(F32) + terms[pair, side, rows_at].astype(F32)
+                        moving[pair, side, rows_at] = value.astype(BF16)
+                        sum_hop(pair, side, h).start()
 
         @pl.when((t >= 6) & (t < pairs + 6))
         def _():
@@ -488,15 +474,11 @@
             pair = lax.rem(pos + 1, pairs)
             give(pos).wait_recv()
             mixed = dot(mix[pair][:, :32], outs[pos])
-            terms[pair, at["core"]] = mixed.astype(BF16).reshape(2, tokens, width)
+            terms[pair] = mixed.astype(BF16).reshape(2, tokens, width)
 
             @pl.when(t == 6)
             def _():
                 own_sum[...] = mixed[:tokens]
-
-            @pl.when(jnp.logical_not(carrier))
-            def _():
-                lend_terms(pair).start()
 
         @pl.when((t >= 2) & (t < pairs + 2))
         def _():
@@ -518,7 +500,7 @@
                     summed[t2].astype(F32)
                     + direct[t2].astype(F32)
                     + parts[at["col"], t2].astype(F32)
-                    + down_bias_ref[...]
+                    + down_bias[...]
                 ).astype(BF16)
                 if p == 1:
                     given[pos] = total
@@ -536,25 +518,12 @@
 
         return carry
 
-    lax.fori_loop(0, pairs + 8, scatter, 0)
-
-    @pl.when(carrier)
-    def _():
-        for b in range(2):
-            for side in range(2):
-                for h in range(CHUNKS):
-                    sum_hop(1, b, side, h).wait_recv()
-                if b == 0:
-                    hand_sum(side).start()
-
-    @pl.when(jnp.logical_not(carrier))
-    def _():
-        for side in range(2):
-            hand_sum(side).wait_recv()
-
-    core = at["core"]
-    total = own_ref[...].astype(F32) + own_sum[...]
-    total = total + moving[0, core, 0].astype(F32) + moving[0, core, 1].astype(F32)
+    lax.fori_loop(0, pairs + 7, scatter, 0)
+
+    for side in range(2):
+        for h in range(CHUNKS):
+            sum_hop(1, side, h).wait_recv()
+    total = own[...] + own_sum[...] + moving[0, 0].astype(F32) + moving[0, 1].astype(F32)
     out_ref[...] = total[:, : out_ref.shape[1]].astype(BF16)
 
     def finish(pos, carry):
@@ -571,55 +540,51 @@
 
     lax.fori_loop(0, pairs, finish, 0)
 
-    @pl.when(carrier)
-    def _():
-        def sent(s, carry):
-            for b in range(2):
-                for side in range(2):
-                    for h in range(CHUNKS):
-                        hop(s, b, side, h).wait_send()
-                        sum_hop(s, b, side, h).wait_send()
-            for side in range(2):
-                hand_block(s, side).wait_send()
-            return carry
-
-        lax.fori_loop(1, pairs, sent, 0)
-        hand_block(0, 1).wait_send()
-        for b in range(2):
+    def sent(s, carry):
+        for side in range(2):
             for h in range(CHUNKS):
-                last_hop(b, last_side(h), h).wait_send()
-                first_sum(b, out_side(h), h).wait_send()
-        for side in range(2):
-            hand_sum(side).wait_send()
-
-    @pl.when(jnp.logical_not(carrier))
-    def _():
-        lend_block().wait_send()
-
-        def lent(pair, carry):
-            lend_terms(pair).wait_send()
-            return carry
-
-        lax.fori_loop(0, pairs, lent, 0)
-
-
-def layer(block, codes, scales, up_bias, low_codes, low_scales, down_bias, own, quarter, ep, tp, top):
-    tokens, width = block.shape
+                hop(s, side, h).wait_send()
+                sum_hop(s, side, h).wait_send()
+        return carry
+
+    lax.fori_loop(1, pairs, sent, 0)
+    for h in range(CHUNKS):
+        last_hop(last_side(h), h).wait_send()
+        first_sum(out_side(h), h).wait_send()
+
+
+def layer(hidden, ids, weights, gain, codes, scales, up_bias, low_codes, low_scales, down_bias, ep, tp):
+    tokens, model_width = hidden.shape
+    top = ids.shape[1]
+    quarter = model_width // tp
+    width = -(-(quarter + 2 * top) // 128) * 128
+    whole_width = -(-model_width // 128) * 128 + 128
     pairs = ep // 4
     word_rows, columns = codes.shape
-    hidden_units, low_lanes = low_codes.shape
+    hidden_units = low_codes.shape[1]
+    low_lanes = -(-low_codes.shape[0] // 128) * 128
+    blocks = low_scales.shape[0]
+    low_parts = max(1, pairs // tp)
     tiles = 2 * pairs
     dma = pltpu.SemaphoreType.DMA
     vmem = pl.BlockSpec(memory_space=pltpu.VMEM)
     hbm = pl.BlockSpec(memory_space=pl.ANY)
-    ring = dma((pairs, 2, 2, CHUNKS))
+    ring = dma((pairs, 2, CHUNKS))
     return pl.pallas_call(
         functools.partial(layer_kernel, ep, tp, top, quarter - (width - 128)),
         out_shape=jax.ShapeDtypeStruct((tokens, quarter), BF16),
-        in_specs=[vmem, hbm, hbm, vmem, hbm, vmem, vmem, vmem],
+        in_specs=[vmem] * 4 + [hbm, hbm, vmem, hbm, hbm, vmem],
         out_specs=vmem,
         scratch_shapes=[
-            pltpu.VMEM((pairs, 2, 2, tokens, width), BF16),
+            pltpu.VMEM((low_lanes, hidden_units), jnp.int32),
+            pltpu.VMEM((tokens, whole_width), F32),
+            pltpu.VMEM((blocks, whole_width), F32),
+            pltpu.VMEM((blocks, model_width), BF16),
+            pltpu.VMEM((tp * low_parts, blocks // low_parts, width), F32),
+            pltpu.VMEM((1, width), F32),
+            pltpu.VMEM((tokens, width), F32),
+            pltpu.VMEM((tokens, width), BF16),
+            pltpu.VMEM((pairs, 2, tokens, width), BF16),
             pltpu.VMEM((pairs, 16, width), BF16),
             pltpu.VMEM((tp, tiles, 16, width), BF16),
             pltpu.VMEM((pairs, 2 * tokens, 128), BF16),
@@ -638,27 +603,18 @@
             pltpu.VMEM((tiles, 16, width), BF16),
             pltpu.VMEM((pairs, 32, width), BF16),
             pltpu.VMEM((pairs, 16, width), BF16),
-            pltpu.VMEM((pairs, 2, 2, tokens, width), BF16),
-            pltpu.VMEM((pairs, 2, 2, tokens, width), BF16),
+            pltpu.VMEM((pairs, 2, tokens, width), BF16),
+            pltpu.VMEM((pairs, 2, tokens, width), BF16),
             pltpu.VMEM((tokens, width), F32),
             dma((4,)),
             ring, ring, dma((pairs,)), dma((pairs,)), dma((tiles, 3)), dma((tiles, 3)),
-            dma((pairs, 2)), dma((pairs, 2)),
             ring, ring, dma((pairs,)), dma((pairs,)), dma((tiles, 3)), dma((tiles, 3)),
-            dma((pairs,)), dma((pairs,)), dma((2,)), dma((2,)),
         ],
         compiler_params=pltpu.CompilerParams(
             collective_id=0, has_side_effects=True, vmem_limit_bytes=60 << 20
         ),
         name="layer",
-    )(block, codes, scales, up_bias, low_codes, low_scales, down_bias, own)
-
-
-def rms_normed(hidden, norm_gain):
-    widened = hidden.astype(F32)
-    mean_square = jnp.mean(widened * widened, axis=-1, keepdims=True)
-    scaled = widened * lax.rsqrt(mean_square + 1e-05) * norm_gain.astype(F32)
-    return scaled.astype(BF16)
+    )(hidden, ids, weights, gain, codes, scales, up_bias, low_codes, low_scales, down_bias)
 
 
 def shards(
@@ -673,37 +629,19 @@
     down_scales,
     down_bias,
 ):
-    ep = lax.axis_size("ep")
-    tp = lax.axis_size("tp")
-    col = lax.axis_index("tp")
-    tokens, model_width = hidden.shape
-    top = route_experts.shape[1]
-    quarter = model_width // tp
-    width = -(-(quarter + 2 * top) // 128) * 128
-    spare = width - quarter
-    normed = rms_normed(hidden, norm_gain)
-    own_normed = lax.dynamic_slice_in_dim(normed, col * quarter, quarter, 1)
-    block = jnp.concatenate(
-        [
-            own_normed,
-            route_experts.astype(BF16),
-            route_weight.astype(BF16),
-            jnp.zeros((tokens, spare - 2 * top), BF16),
-        ],
-        axis=1,
-    )
-    hidden_units = down_codes.shape[1]
-    low_codes = jnp.pad(down_codes[0], ((0, 0), (0, -(down_codes.shape[2]) % 128)))
-    low_parts = max(1, ep // 4 // tp)
-    low_scales = 0.5 * down_scales[0].astype(F32).reshape(-1, tp, quarter)
-    low_scales = jnp.pad(jnp.moveaxis(low_scales, 1, 0), ((0, 0), (0, 0), (0, spare)))
-    low_scales = low_scales.reshape(tp * low_parts, hidden_units // 32 // low_parts, width)
-    bias = jnp.pad(down_bias.astype(F32), ((0, 0), (0, spare)))
-    own = lax.dynamic_slice_in_dim(hidden, col * quarter, quarter, 1)
-    own = jnp.pad(own, ((0, 0), (0, spare)))
     return layer(
-        block, gate_up_codes[0], gate_up_scales[0], gate_up_bias.astype(F32), low_codes, low_scales, bias, own,
-        quarter, ep, tp, top,
+        hidden,
+        route_experts,
+        route_weight,
+        norm_gain[None],
+        gate_up_codes[0],
+        gate_up_scales[0],
+        gate_up_bias,
+        down_codes[0].T,
+        down_scales[0],
+        down_bias,
+        lax.axis_size("ep"),
+        lax.axis_size("tp"),
     )
 
 

time: 198 us -> 193 us (0.975)
  other arithmetic: 5.74 us -> 0 us
  Pallas kernels: 185 us -> 187 us
    convert_element_type x5 -> x0, other arithmetic: 3.23 us -> none  [the longest x1 1.04 us: rms_normed(): widened = hidden.astype(F32)]
    unnamed x10 -> x3, local copies, waits for them, and re-layouts: 1.88 us -> 4.3 us
    pallas_call x1, Pallas kernels: 185 us -> 187 us  [layer(): pl.pallas_call(functools.partial(layer_kernel, ep, tp, top, quarter - (wi...]
where the time goes in v3:
time: 193 us
  Pallas kernels  187 us (97%)
  local copies, waits for them, and re-layouts  5.59 us (3%)
    pallas_call x1, Pallas kernels, layer(): pl.pallas_call(functools.partial(layer_kernel, ep, tp, top, quarter - (wi...  187 us
    unnamed x3, local copies, waits for them, and re-layouts  4.3 us

profile of v3, /device:TPU:33, one launch (start us, length us, event | category | flops | bytes accessed | tf_op | source)
XLA Modules:
  0.0 192.9 jit_solution(15761082976173808368)
XLA Ops:
  0.0 1.3 broadcast_in_dim.3.gain_ref
  1.3 1.4 copy.11.ids_ref
  2.7 1.4 copy.12.weights_ref
  4.1 187.3 %layer.1 = bf16[64,720]{1,0:T(8,128)(2,1)} custom-call(bf16[64,2880]{1,0:T(8,128)(2,1)} %hidden_ref.1, s32[64,4]{1,0:T(8,128)} %copy.11.ids_ref, f32[64,4]{1,0:T(8,128)} %copy.12.weights_ref, bf16[1,2880]{1,0:T(2,128)(2,1)} %broadcast_in_dim.3.gain_ref, s32[360,1280]{1,0:T(8,128)} %bitcast.6, bf16[90,1280]{1,0:T(8,128)(2,1)} %bitcast.8, ...), custom_call_target="tpu_custom_call" | custom-call | tf_op jit(solution)/shard_map/layer/pallas_call | solution.py:573
  191.4 1.5 copy.14

commit v4 on v3

--- a/solution.py
+++ b/solution.py
@@ -41,7 +41,7 @@
     barrier = pltpu.get_barrier_semaphore()
     for place in ({"ep": at["up"]}, {"ep": at["down"]}, {"ep": at["pal"]}, {"tp": at["right"]}, {"tp": at["left"]}):
         pl.semaphore_signal(barrier, inc=1, device_id=place, device_id_type=pl.DeviceIdType.MESH)
-    pl.semaphore_wait(barrier, 5)
+    return barrier
 
 
 def remote(src, dst, send, recv, place):
@@ -80,6 +80,7 @@
     real_units = word_rows // 2 // tp
     words = real_units * 2
     at = neighbours(ep, tp)
+    barrier = greet(at)
 
     fetches = [
         pltpu.make_async_copy(codes_hbm, codes, local_sem.at[1]),
@@ -112,7 +113,7 @@
         block_ref[:, : width - 128] = normed[:, : width - 128].astype(BF16)
     is_data = iota((tokens, 128), 1) < meta_at
     block_ref[:, width - 128 :] = jnp.where(is_data, normed[:, width - 128 :], meta_own).astype(BF16)
-    greet(at)
+    pl.semaphore_wait(barrier, 5)
 
     def piece(pair, side, h):
         return held.at[pair, side, pl.ds(h * part, part)]
@@ -289,6 +290,38 @@
             relayed(pos, p).wait_recv()
         return carry
 
+    def x_action(i, u):
+        if i < 2:
+
+            @pl.when((u >= 1) & (u < pairs + 1))
+            def _():
+                (go_right if i == 0 else go_left)(u - 1, 0).start()
+
+        elif i < 4:
+
+            @pl.when((u >= 2) & (u < pairs + 2))
+            def _():
+                if i == 2:
+                    to_pal(u - 2).wait_recv()
+                (go_right if i == 2 else go_left)(u - 2, 1).start()
+
+        elif i == 4:
+
+            @pl.when((u >= 3) & (u < pairs + 3))
+            def _():
+                from_left(u - 3, 0).wait_recv()
+                relay(u - 3, 0).start()
+
+        else:
+
+            @pl.when(u >= 4)
+            def _():
+                from_right(u - 4, 1).wait_recv()
+                relay(u - 4, 1).start()
+
+    def spread_out(n, count):
+        return range(count * n // (2 * CHUNKS), count * (n + 1) // (2 * CHUNKS))
+
     def gather(u, carry):
         @pl.when(u < pairs - 1)
         def _():
@@ -307,6 +340,14 @@
                         def _():
                             last_hop(side, h).start()
 
+                    for i in spread_out(2 * h + side, 6):
+                        x_action(i, u)
+
+        @pl.when(u >= pairs - 1)
+        def _():
+            for i in range(6):
+                x_action(i, u)
+
         @pl.when(u == pairs - 1)
         def _():
             for h in range(CHUNKS):
@@ -327,21 +368,6 @@
         def _():
             select(lax.rem(u + 1, pairs), u)
             to_pal(u).start()
-            go_right(u, 0).start()
-            go_left(u, 0).start()
-
-        @pl.when((u >= lag) & (u < pairs + lag))
-        def _():
-            to_pal(u - lag).wait_recv()
-            go_right(u - lag, 1).start()
-            go_left(u - lag, 1).start()
-            from_left(u - lag, 0).wait_recv()
-            relay(u - lag, 0).start()
-
-        @pl.when(u >= 2 * lag)
-        def _():
-            from_right(u - 2 * lag, 1).wait_recv()
-            relay(u - 2 * lag, 1).start()
 
         @pl.when(u < pairs)
         def _():
@@ -425,15 +451,26 @@
         for q in range(tp):
             project_down(q, 0)
 
+    def sum_action(i, t):
+        if i < 4:
+
+            @pl.when(t < pairs)
+            def _():
+                p = i % 2
+                (two_away if i < 2 else one_away)((pairs - 1 - t) * 2 + p, p).start()
+
+        else:
+
+            @pl.when((t >= 2) & (t < pairs + 2))
+            def _():
+                p = i - 4
+                t1 = (pairs + 1 - t) * 2 + p
+                two_away(t1, p).wait_recv()
+                col = at["right"] if p == 0 else at["left"]
+                staged[t1] = (across[t1].astype(F32) + parts[col, t1].astype(F32)).astype(BF16)
+                onward(t1, p).start()
+
     def scatter(t, carry):
-        @pl.when(t < pairs)
-        def _():
-            pos = pairs - 1 - t
-            for p in range(2):
-                two_away(pos * 2 + p, p).start()
-            for p in range(2):
-                one_away(pos * 2 + p, p).start()
-
         @pl.when(t >= 7)
         def _():
             u = t - 7
@@ -467,6 +504,13 @@
                         value = moving[pair, side, rows_at].astype(F32) + terms[pair, side, rows_at].astype(F32)
                         moving[pair, side, rows_at] = value.astype(BF16)
                         sum_hop(pair, side, h).start()
+                        for i in spread_out(2 * h + (side != out_side(h)), 6):
+                            sum_action(i, t)
+
+        @pl.when(t < 8)
+        def _():
+            for i in range(6):
+                sum_action(i, t)
 
         @pl.when((t >= 6) & (t < pairs + 6))
         def _():
@@ -479,15 +523,6 @@
             @pl.when(t == 6)
             def _():
                 own_sum[...] = mixed[:tokens]
-
-        @pl.when((t >= 2) & (t < pairs + 2))
-        def _():
-            for p in range(2):
-                t1 = (pairs + 1 - t) * 2 + p
-                two_away(t1, p).wait_recv()
-                col = at["right"] if p == 0 else at["left"]
-                staged[t1] = (across[t1].astype(F32) + parts[col, t1].astype(F32)).astype(BF16)
-                onward(t1, p).start()
 
         @pl.when((t >= 4) & (t < pairs + 4))
         def _():

time: 193 us -> 192 us (level)
  no operation moved by 1% of the time
where the time goes in v4:
time: 192 us
  Pallas kernels  186 us (97%)
  local copies, waits for them, and re-layouts  5.59 us (3%)
    pallas_call x1, Pallas kernels, layer(): pl.pallas_call(functools.partial(layer_kernel, ep, tp, top, quarter - (wi...  186 us
    unnamed x3, local copies, waits for them, and re-layouts  4.3 us

profile of v4, /device:TPU:33, one launch (start us, length us, event | category | flops | bytes accessed | tf_op | source)
XLA Modules:
  0.0 192.0 jit_solution(3462067891510961880)
XLA Ops:
  0.0 1.3 broadcast_in_dim.3.gain_ref
  1.3 1.4 copy.11.ids_ref
  2.7 1.4 copy.12.weights_ref
  4.1 186.4 %layer.1 = bf16[64,720]{1,0:T(8,128)(2,1)} custom-call(bf16[64,2880]{1,0:T(8,128)(2,1)} %hidden_ref.1, s32[64,4]{1,0:T(8,128)} %copy.11.ids_ref, f32[64,4]{1,0:T(8,128)} %copy.12.weights_ref, bf16[1,2880]{1,0:T(2,128)(2,1)} %broadcast_in_dim.3.gain_ref, s32[360,1280]{1,0:T(8,128)} %bitcast.6, bf16[90,1280]{1,0:T(8,128)(2,1)} %bitcast.8, ...), custom_call_target="tpu_custom_call" | custom-call | tf_op jit(solution)/shard_map/layer/pallas_call | solution.py:608
  190.5 1.5 copy.14
